TPU v7x, 512 devices: a whole 4x4x16 slice. The times are simulated.
512 devices in a mesh: dp: 64 (over z, x_lo, core), mp: 8 (over y, x_hi).
Axes of the slice: x: 4 (x_hi: 2, x_lo: 2; x = x_hi * 2 + x_lo), y: 4, z: 16, core: 2. Of those that a mesh axis runs over, the one named last changes fastest.
Arguments:
- inputs_store: bfloat16 [512, 128], replicated, may hold values from -6 to 6
- window: int32 [64], replicated, may hold values from 0 to 511
- targets_store: bfloat16 [512, 4096], P(None, ('dp', 'mp')), may hold values from -6 to 6
- jac_store: bfloat16 [512, 4096, 128], P(None, ('dp', 'mp')), may hold values from -4 to 4
- first_weight: bfloat16 [128, 1024], replicated, may hold values from -0.5 to 0.5
- first_bias: bfloat16 [1024], replicated, may hold values from -3 to 3
- hidden_weight: bfloat16 [1024, 1024], P(None, 'mp'), may hold values from -0.1875 to 0.1875
- hidden_bias: bfloat16 [1024], P('mp'), may hold values from -3 to 3
- decoder_weight: bfloat16 [4096, 1024], P(('dp', 'mp')), may hold values from -0.1875 to 0.1875
Outputs:
- first_weights: float32 [128, 1024], replicated
- first_biases: float32 [1024], replicated
- hidden_weights: float32 [1024, 1024], P(None, 'mp')
- hidden_biases: float32 [1024], P('mp')
- decoder_grad: float32 [4096, 1024], P(('dp', 'mp'))
Inputs may be any that keep to these rules, and one draw needn't show every extreme that they name: `window`: indices of stored samples; an index may repeat.
All inputs are finite; a program needn't handle non-finite values.
Results may differ from a plain program's by a relative error of at most 0.011.
Values may be sent and summed in bfloat16 or wider, within the bound.
A program may use at most 64 MiB of HBM per device.

v0:
```python
import jax
import jax.numpy as jnp
from jax import lax
from jax.sharding import Mesh
from jax.sharding import PartitionSpec as P

DP = ("dp_0", "dp_1", "dp_2")
DP_MP = ("dp_0", "dp_1", "dp_2", "mp")


def side_by_side(arrays, axis, split_dim, concat_dim, along):
    columns = [a.reshape(*a.shape[:along], -1) for a in arrays]
    both = jnp.concatenate(columns, axis=along)
    out, at, gathered = (
        lax.all_to_all(both, axis, split_axis=split_dim, concat_axis=concat_dim, tiled=True),
        0,
        [],
    )
    for a, column in zip(arrays, columns):
        piece = out[..., at : at + column.shape[along]]
        gathered.append(piece.reshape(*piece.shape[:along], *a.shape[along:]))
        at += column.shape[along]
    return tuple(gathered)


def rows_first(arrays, axis, dims):
    turned = [jnp.moveaxis(a, dim, 0) for a, dim in zip(arrays, dims)]
    widths = [t[0].size for t in turned]
    both = jnp.concatenate([t.reshape(-1, w) for t, w in zip(turned, widths)], axis=1)
    out = lax.all_gather(both, axis, axis=0, tiled=True)
    pieces = jnp.split(out, [sum(widths[:k]) for k in range(1, len(widths))], axis=1)
    return tuple(
        (
            jnp.moveaxis(b.reshape(-1, *t.shape[1:]), 0, dim)
            for b, t, dim in zip(pieces, turned, dims)
        )
    )


def copy_for_each(shard, axis):
    copies = jnp.broadcast_to(shard, (lax.axis_size(axis), *shard.shape))
    return lax.all_to_all(copies, axis, split_axis=0, concat_axis=0, tiled=True)


def in_order(pieces, dim):
    pieces = jnp.moveaxis(pieces, 0, dim)
    shape = pieces.shape
    return pieces.reshape(*shape[:dim], shape[dim] * shape[dim + 1], *shape[dim + 2 :])


def gathered_copies(shard, axis, dim):
    pieces = copy_for_each(shard, axis)
    return in_order(pieces, dim)


def cut_along(shard, dim, size):
    before, after = (shard.shape[:dim], shard.shape[dim + 1 :])
    return jnp.moveaxis(shard.reshape(*before, size, -1, *after), dim, 0)


def sum_at_owner(shard, axis, dim):
    size = lax.axis_size(axis)
    pieces = lax.all_to_all(cut_along(shard, dim, size), axis, 0, 0, tiled=True)
    return jnp.sum(pieces, axis=0)


def summed_rows(shard, axes, dim):
    far, near = axes
    pieces = cut_along(shard, dim, lax.axis_size(far))
    nearer = sum_at_owner(pieces, near, dim + 1)
    arrived = lax.all_to_all(nearer, far, split_axis=0, concat_axis=0, tiled=True)
    return arrived.sum(axis=0)


def sent_and_summed(shard, axis, dim):
    pieces = cut_along(shard, dim, lax.axis_size(axis))
    arrived = lax.all_to_all(pieces, axis, split_axis=0, concat_axis=0, tiled=True)
    return arrived.astype(jnp.float32).sum(axis=0)


def of_everyone(shard, axis):
    return copy_for_each(shard, axis).astype(jnp.float32).sum(axis=0)


def padded_to(lines, size):
    spare = -lines.shape[0] % size
    if not spare:
        return lines
    return jnp.concatenate([lines, jnp.zeros((spare, *lines.shape[1:]), lines.dtype)])


def whole_of(shard, axes, dim):
    far, near = axes
    first = copy_for_each(shard, far)
    pieces = jnp.swapaxes(copy_for_each(first, near), 0, 1)
    return in_order(pieces.reshape(-1, *shard.shape), dim)


def sum_by_parts(shard, axes):
    own = summed_rows(padded_to(shard, lax.axis_size(axes[0]) * lax.axis_size(axes[1])), axes, 0)
    whole = whole_of(own, axes, 0)
    return whole[: len(shard)].reshape(shard.shape)


def together(arrays, axis):
    ends = [0]
    for a in arrays:
        ends.append(ends[-1] + a.size)
    subtotal = sum_by_parts(jnp.concatenate([a.ravel() for a in arrays]), axis)
    return tuple((subtotal[b:e].reshape(a.shape) for a, b, e in zip(arrays, ends, ends[1:])))


def on_device(
    inputs_store,
    window,
    targets_store,
    jac_store,
    first_weight,
    first_bias,
    hidden_weight,
    hidden_bias,
    decoder_weight,
):
    each_count = window.shape[0] // lax.axis_size(DP)
    jac_window = jac_store[window]
    target_window = targets_store[window]
    jac_mine, target_mine = side_by_side((jac_window, target_window), DP, 0, 1, 2)
    mine_index = lax.dynamic_slice_in_dim(window, lax.axis_index(DP) * each_count, each_count)
    inputs = inputs_store[mine_index]
    weight_one = first_weight.astype(jnp.float32)
    first_pre = jnp.dot(
        inputs, first_weight, preferred_element_type=jnp.float32
    ) + first_bias.astype(jnp.float32)
    first_act = jnp.tanh(first_pre)
    first_slope = 1.0 - first_act * first_act
    first_tan = (first_slope[:, None, :] * weight_one[None]).astype(jnp.bfloat16)
    first_round = first_act.astype(jnp.bfloat16)
    hidden_lin = jnp.einsum(
        "srh,hk->srk", first_tan, hidden_weight, preferred_element_type=jnp.float32
    )
    hidden_pre = jnp.dot(
        first_round, hidden_weight, preferred_element_type=jnp.float32
    ) + hidden_bias.astype(jnp.float32)
    hidden_act = jnp.tanh(hidden_pre)
    hidden_slope = 1.0 - hidden_act * hidden_act
    hidden_tangent = (hidden_slope[:, None, :] * hidden_lin).astype(jnp.bfloat16)
    hidden_rounded_state = hidden_act.astype(jnp.bfloat16)
    act_all, tangent_full_rows = rows_first((hidden_rounded_state, hidden_tangent), "mp", (1, 2))
    decoder_full_rows = gathered_copies(decoder_weight, DP, 0)
    outputs_net = jnp.einsum(
        "sk,ok->so", act_all, decoder_full_rows, preferred_element_type=jnp.float32
    )
    jacobian_predicted = jnp.einsum(
        "mvn,an->mav", tangent_full_rows, decoder_full_rows, preferred_element_type=jnp.float32
    )
    output_residual = (outputs_net - target_mine.astype(jnp.float32)).astype(jnp.bfloat16)
    jacobian_residual = (jacobian_predicted - jac_mine.astype(jnp.float32)).astype(jnp.bfloat16)
    decoder_grad = summed_rows(
        jnp.einsum("qi,qm->im", output_residual, act_all, preferred_element_type=jnp.float32)
        + jnp.einsum(
            "hzy,hym->zm", jacobian_residual, tangent_full_rows, preferred_element_type=jnp.float32
        ),
        (("dp_0", "dp_1"), "dp_2"),
        0,
    )
    act_partial = jnp.einsum(
        "so,oh->sh", output_residual, decoder_full_rows, preferred_element_type=jnp.float32
    )
    tan_partial = jnp.einsum(
        "lud,uf->ldf", jacobian_residual, decoder_full_rows, preferred_element_type=jnp.float32
    )
    act_back, tan_back = (
        sent_and_summed(act_partial.astype(jnp.bfloat16), "mp", 1),
        sent_and_summed(tan_partial.astype(jnp.bfloat16), "mp", 2),
    )
    lin_back = tan_back * hidden_slope[:, None, :]
    pre_back = act_back * hidden_slope - 2.0 * hidden_act * hidden_slope * jnp.sum(
        tan_back * hidden_lin, axis=1
    )
    lin_round = lin_back.astype(jnp.bfloat16)
    pre_round = pre_back.astype(jnp.bfloat16)
    hidden_grad = jnp.einsum(
        "sh,sk->hk", first_round, pre_round, preferred_element_type=jnp.float32
    ) + jnp.einsum("srh,srk->hk", first_tan, lin_round, preferred_element_type=jnp.float32)
    hidden_bgrad = jnp.sum(pre_back, axis=0)
    tan_lower = jnp.einsum(
        "srk,hk->srh", lin_round, hidden_weight, preferred_element_type=jnp.float32
    )
    act_lower = jnp.einsum(
        "sk,hk->sh", pre_round, hidden_weight, preferred_element_type=jnp.float32
    )
    pre_lower = act_lower * first_slope - 2.0 * first_act * first_slope * jnp.sum(
        tan_lower * weight_one[None], axis=1
    )
    weight_part = jnp.einsum(
        "sr,sh->rh", inputs.astype(jnp.float32), pre_lower, precision=lax.Precision.HIGHEST
    ) + jnp.sum(tan_lower * first_slope[:, None, :], axis=0)
    bias_part = jnp.sum(pre_lower, axis=0)
    weight_mid, bias_mid = (
        of_everyone(weight_part.astype(jnp.bfloat16), "mp").astype(jnp.float32),
        of_everyone(bias_part.astype(jnp.bfloat16), "mp").astype(jnp.float32),
    )
    first_weights, first_biases, hidden_weights, hidden_biases = together(
        (weight_mid, bias_mid, hidden_grad, hidden_bgrad), (("dp_0", "dp_1"), "dp_2")
    )
    return (first_weights, first_biases, hidden_weights, hidden_biases, decoder_grad)


def solution(mesh):
    torus = Mesh(mesh.devices.reshape(16, 2, 2, mesh.shape["mp"]), ("dp_0", "dp_1", "dp_2", "mp"))
    return jax.shard_map(
        on_device,
        mesh=torus,
        in_specs=(
            P(),
            P(),
            P(None, DP_MP),
            P(None, DP_MP, None),
            P(),
            P(),
            P(None, "mp"),
            P("mp"),
            P(DP_MP, None),
        ),
        out_specs=(P(), P(), P(None, "mp"), P("mp"), P(DP_MP, None)),
        check_vma=False,
    )
```

profile of v0, /device:TPU:1, one launch (start us, length us, event | category | flops | bytes accessed | tf_op | source)
XLA Modules:
  0.0 343.3 jit_solution(15501637237382968844)
XLA Ops:
  0.7 0.7 compare_select_fusion
  1.4 0.9 copy.57
  2.3 0.6 gather_fusion
  2.9 0.6 gather_fusion.1
  3.5 0.5 copy.58
  4.1 40.1 %all_to_all.76 = bf16[64,8,129]{2,1,0:T(8,128)(2,1)S(1)} all-to-all(bf16[64,8,129]{2,1,0:T(8,128)(2,1)S(1)} %pad_maximum_fusion.1), channel_id=1, replica_groups=mesh['dp_0'=16,'dp_1'=2,'dp_2'=2,'mp'=8] {'dp_0','dp_1','dp_2'}, dimensions={0} | all-to-all | bytes 264192 | tf_op jit(solution)/shard_map/all_to_all | solution.py:15
  44.2 1.1 broadcast_in_dim.15
  45.3 4.8 %all-to-all-start = ((bf16[64,8,1024]{2,1,0:T(8,128)(2,1)}), bf16[64,8,1024]{2,1,0:T(8,128)(2,1)S(1)}, u32[]{:S(2)}, u32[]{:S(2)}) async-start(bf16[64,8,1024]{2,1,0:T(8,128)(2,1)} %broadcast_in_dim.15), calls=%async_computation | async-start | bytes 2097152 | tf_op jit(solution)/shard_map/all_to_all | solution.py:42
  50.2 0.6 dynamic_slice.3
  52.7 0.8 fusion.24
  54.0 0.3 copy-done.17
  54.3 29.2 %all_gather.3 = bf16[1024,129]{0,1:T(8,128)(2,1)S(1)} all-gather(bf16[128,129]{0,1:T(8,128)(2,1)S(1)} %pad_maximum_fusion.2), channel_id=1, replica_groups=mesh['dp_0'=16,'dp_1'=2,'dp_2'=2,'mp'=8] {'mp'}, dimensions={0}, use_global_device_ids=true | all-gather | bytes 297216 | tf_op jit(solution)/shard_map/all_gather | solution.py:30
  83.7 20.4 %all-to-all-done = bf16[64,8,1024]{2,1,0:T(8,128)(2,1)S(1)} async-done(((bf16[64,8,1024]{2,1,0:T(8,128)(2,1)}), bf16[64,8,1024]{2,1,0:T(8,128)(2,1)S(1)}, u32[]{:S(2)}, u32[]{:S(2)}) %all-to-all-start) | async-done | bytes 1048608 | tf_op jit(solution)/shard_map/all_to_all | solution.py:42
  104.2 0.4 fusion.11
  104.5 0.6 fusion.27
  105.1 0.2 fusion.9
  105.4 0.6 copy.59
  106.0 6.4 %all-to-all-start.2 = ((bf16[8,1,128]{2,1,0:T(2,128)(2,1)}), bf16[8,1,128]{2,1,0:T(2,128)(2,1)S(1)}, u32[]{:S(2)}, u32[]{:S(2)}) async-start(bf16[8,1,128]{2,1,0:T(2,128)(2,1)} %copy.59), calls=%async_computation.2 | async-start | bytes 8192 | tf_op jit(solution)/shard_map/all_to_all | solution.py:77
  112.4 0.5 fusion.4
  112.9 0.3 fusion.1
  113.2 0.7 copy.77
  114.0 4.8 %all-to-all-done.2 = bf16[8,1,128]{2,1,0:T(2,128)(2,1)S(1)} async-done(((bf16[8,1,128]{2,1,0:T(2,128)(2,1)}), bf16[8,1,128]{2,1,0:T(2,128)(2,1)S(1)}, u32[]{:S(2)}, u32[]{:S(2)}) %all-to-all-start.2) | async-done | bytes 2080 | tf_op jit(solution)/shard_map/all_to_all | solution.py:77
  118.8 3.4 all-to-all-start.3
  122.2 0.7 bitcast_convert_fusion
  123.0 6.9 %all-to-all-done.3 = bf16[8,1,128,128]{3,2,1,0:T(8,128)(2,1)S(1)} async-done(((bf16[8,1,128,128]{3,2,1,0:T(8,128)(2,1)}), bf16[8,1,128,128]{3,2,1,0:T(8,128)(2,1)S(1)}, u32[]{:S(2)}, u32[]{:S(2)}) %all-to-all-start.3) | async-done | bytes 262176 | tf_op jit(solution)/shard_map/all_to_all | solution.py:77
  130.2 0.5 convert_convert_fusion
  130.8 0.3 copy-done.12
  131.2 0.5 broadcast.74
  131.7 0.7 reduce.12
  132.5 0.6 reshape.262
  133.1 3.3 all-to-all-start.5
  136.6 6.4 %all-to-all-done.5 = bf16[8,2,512]{2,1,0:T(2,128)(2,1)S(1)} async-done(((bf16[8,2,512]{2,1,0:T(2,128)(2,1)}), bf16[8,2,512]{2,1,0:T(2,128)(2,1)S(1)}, u32[]{:S(2)}, u32[]{:S(2)}) %all-to-all-start.5) | async-done | bytes 16416 | tf_op jit(solution)/shard_map/all_to_all | solution.py:42
  142.9 1.6 broadcast_in_dim.33
  144.5 3.7 %all-to-all-start.4 = ((bf16[8,128,1024]{2,1,0:T(8,128)(2,1)}), bf16[8,128,1024]{2,1,0:T(8,128)(2,1)S(1)}, u32[]{:S(2)}, u32[]{:S(2)}) async-start(bf16[8,128,1024]{2,1,0:T(8,128)(2,1)} %broadcast_in_dim.33), calls=%async_computation.4 | async-start | bytes 4194304 | tf_op jit(solution)/shard_map/all_to_all | solution.py:42
  148.3 0.7 slice_reduce_fusion
  149.0 1.4 multiply_add_fusion
  150.5 1.5 copy.75
  152.0 1.1 fusion
  153.1 17.2 %all-to-all-done.4 = bf16[8,128,1024]{2,1,0:T(8,128)(2,1)S(1)} async-done(((bf16[8,128,1024]{2,1,0:T(8,128)(2,1)}), bf16[8,128,1024]{2,1,0:T(8,128)(2,1)S(1)}, u32[]{:S(2)}, u32[]{:S(2)}) %all-to-all-start.4) | async-done | bytes 2097184 | tf_op jit(solution)/shard_map/all_to_all | solution.py:42
  170.3 0.3 convert_reduce_fusion
  170.8 0.9 copy-done.4
  171.8 1.1 reshape_reshape.9
  173.0 12.4 %all_to_all.77 = f32[2,32,4114]{2,1,0:T(8,128)} all-to-all(f32[2,32,4114]{2,1,0:T(8,128)S(1)} %copy.63), channel_id=1, replica_groups=mesh['dp_0'=16,'dp_1'=2,'dp_2'=2,'mp'=8] {'dp_2'}, dimensions={0} | all-to-all | bytes 2106368 | tf_op jit(solution)/shard_map/all_to_all | solution.py:63
  185.4 4.1 %all-to-all-start.10 = ((f32[2,32,8,1024]{3,2,1,0:T(8,128)}), f32[2,32,8,1024]{3,2,1,0:T(8,128)S(1)}, u32[]{:S(2)}, u32[]{:S(2)}) async-start(f32[2,32,8,1024]{3,2,1,0:T(8,128)} %bitcast.86), calls=%async_computation.10 | async-start | bytes 4194304 | tf_op jit(solution)/shard_map/all_to_all | solution.py:63
  189.5 2.2 reduce_sum.108
  191.7 2.2 all_to_all.57
  193.9 6.1 %all-to-all-start.7 = ((f32[32,1,4114]{2,1,0:T(1,128)}), f32[32,1,4114]{2,1,0:T(1,128)}, u32[]{:S(2)}, u32[]{:S(2)}) async-start(f32[32,1,4114]{2,1,0:T(1,128)} %all_to_all.57), calls=%async_computation.7 | async-start | bytes 1081344 | tf_op jit(solution)/shard_map/all_to_all | solution.py:71
  200.0 1.2 reduce_sum.110
  201.2 31.8 %all-to-all-done.7 = f32[32,1,4114]{2,1,0:T(1,128)} async-done(((f32[32,1,4114]{2,1,0:T(1,128)}), f32[32,1,4114]{2,1,0:T(1,128)}, u32[]{:S(2)}, u32[]{:S(2)}) %all-to-all-start.7) | async-done | bytes 526624 | tf_op jit(solution)/shard_map/all_to_all | solution.py:71
  232.9 4.1 %all-to-all-start.11 = ((f32[32,8,1024]{2,1,0:T(8,128)}), f32[32,8,1024]{2,1,0:T(8,128)S(1)}, u32[]{:S(2)}, u32[]{:S(2)}) async-start(f32[32,8,1024]{2,1,0:T(8,128)} %reduce_sum.110), calls=%async_computation.11 | async-start | bytes 2097152 | tf_op jit(solution)/shard_map/all_to_all | solution.py:71
  237.1 1.4 reduce_sum.109
  238.5 51.7 %all-to-all-done.11 = f32[32,8,1024]{2,1,0:T(8,128)S(1)} async-done(((f32[32,8,1024]{2,1,0:T(8,128)}), f32[32,8,1024]{2,1,0:T(8,128)S(1)}, u32[]{:S(2)}, u32[]{:S(2)}) %all-to-all-start.11) | async-done | bytes 1048608 | tf_op jit(solution)/shard_map/all_to_all | solution.py:71
  290.2 1.1 broadcast_in_dim.35
  291.3 5.5 %all-to-all-start.8 = ((f32[32,1,4114]{2,1,0:T(1,128)}), f32[32,1,4114]{2,1,0:T(1,128)S(1)}, u32[]{:S(2)}, u32[]{:S(2)}) async-start(f32[32,1,4114]{2,1,0:T(1,128)} %broadcast_in_dim.35), calls=%async_computation.8 | async-start | bytes 1081344 | tf_op jit(solution)/shard_map/all_to_all | solution.py:42
  296.8 0.7 reduce_sum.111
  297.5 30.8 %all-to-all-done.8 = f32[32,1,4114]{2,1,0:T(1,128)S(1)} async-done(((f32[32,1,4114]{2,1,0:T(1,128)}), f32[32,1,4114]{2,1,0:T(1,128)S(1)}, u32[]{:S(2)}, u32[]{:S(2)}) %all-to-all-start.8) | async-done | bytes 526624 | tf_op jit(solution)/shard_map/all_to_all | solution.py:42
  328.5 7.4 %all_to_all.78 = f32[2,32,4114]{2,1,0:T(8,128)S(1)} all-to-all(f32[2,32,4114]{2,1,0:T(8,128)S(1)} %broadcast_in_dim.36), channel_id=1, replica_groups=mesh['dp_0'=16,'dp_1'=2,'dp_2'=2,'mp'=8] {'dp_2'}, dimensions={0} | all-to-all | bytes 2106368 | tf_op jit(solution)/shard_map/all_to_all | solution.py:42
  335.9 0.8 copy.64
  336.7 0.9 reshape_reshape.10
  337.6 1.8 slice.25
  339.4 0.5 slice.44
  340.0 0.6 slice.42
  340.6 1.9 slice.43
  342.5 0.9 reshape.209
  (74 shorter events, 2.0 us)
Async XLA Ops:
  0.6 1.6 copy-start
  0.6 43.6 %copy-start.9 = (bf16[8,1024]{1,0:T(8,128)(2,1)S(1)}, bf16[8,1024]{1,0:T(8,128)(2,1)}, u32[]{:S(2)}) copy-start(bf16[8,1024]{1,0:T(8,128)(2,1)} %param.17) | copy-start | bytes 49156
  45.3 4.9 %copy-start.21 = (s32[64]{0:T(128)S(1)}, s32[64]{0:T(128)}, u32[]{:S(2)}) copy-start(s32[64]{0:T(128)} %param.10) | copy-start | bytes 772
  45.3 7.4 %copy-start.2 = (bf16[128,1024]{1,0:T(8,128)(2,1)S(1)}, bf16[128,1024]{1,0:T(8,128)(2,1)}, u32[]{:S(2)}) copy-start(bf16[128,1024]{1,0:T(8,128)(2,1)} %param.13) | copy-start | bytes 786436
  45.3 8.2 %copy-start.10 = (bf16[1024]{0:T(1024)(128)(2,1)S(1)}, bf16[1024]{0:T(1024)(128)(2,1)}, u32[]{:S(2)}) copy-start(bf16[1024]{0:T(1024)(128)(2,1)} %param.14) | copy-start | bytes 6148
  45.3 8.3 %copy-start.1 = (bf16[1024,128]{1,0:T(8,128)(2,1)S(1)}, bf16[1024,128]{1,0:T(8,128)(2,1)}, u32[]{:S(2)}) copy-start(bf16[1024,128]{1,0:T(8,128)(2,1)} %param.15) | copy-start | bytes 786436
  45.3 8.3 %copy-start.20 = (bf16[128]{0:T(256)(128)(2,1)S(1)}, bf16[128]{0:T(256)(128)(2,1)}, u32[]{:S(2)}) copy-start(bf16[128]{0:T(256)(128)(2,1)} %param.16) | copy-start | bytes 772
  45.3 58.8 %all-to-all-start = ((bf16[64,8,1024]{2,1,0:T(8,128)(2,1)}), bf16[64,8,1024]{2,1,0:T(8,128)(2,1)S(1)}, u32[]{:S(2)}, u32[]{:S(2)}) async-start(bf16[64,8,1024]{2,1,0:T(8,128)(2,1)} %broadcast_in_dim.15), calls=%async_computation | async-start | bytes 2097152 | tf_op jit(solution)/shard_map/all_to_all | solution.py:42
  53.7 0.5 copy-start.17
  53.8 0.5 copy-start.14
  83.5 28.9 %copy-start.3 = (bf16[1024,129]{0,1:T(8,128)(2,1)}, bf16[1024,129]{0,1:T(8,128)(2,1)S(1)}, u32[]{:S(2)}) copy-start(bf16[1024,129]{0,1:T(8,128)(2,1)S(1)} %all_gather.3) | copy-start | bytes 792580
  106.0 12.8 %all-to-all-start.2 = ((bf16[8,1,128]{2,1,0:T(2,128)(2,1)}), bf16[8,1,128]{2,1,0:T(2,128)(2,1)S(1)}, u32[]{:S(2)}, u32[]{:S(2)}) async-start(bf16[8,1,128]{2,1,0:T(2,128)(2,1)} %copy.59), calls=%async_computation.2 | async-start | bytes 8192 | tf_op jit(solution)/shard_map/all_to_all | solution.py:77
  113.2 16.7 %copy-start.15 = (f32[128]{0:T(128)S(1)}, f32[128]{0:T(128)}, u32[]{:S(2)}) copy-start(f32[128]{0:T(128)} %copy-done.14) | copy-start | bytes 1540
  114.0 16.2 %copy-start.18 = (f32[128]{0:T(128)S(1)}, f32[128]{0:T(128)}, u32[]{:S(2)}) copy-start(f32[128]{0:T(128)} %copy-done.17) | copy-start | bytes 1540
  118.8 11.0 %all-to-all-start.3 = ((bf16[8,1,128,128]{3,2,1,0:T(8,128)(2,1)}), bf16[8,1,128,128]{3,2,1,0:T(8,128)(2,1)S(1)}, u32[]{:S(2)}, u32[]{:S(2)}) async-start(bf16[8,1,128,128]{3,2,1,0:T(8,128)(2,1)} %bitcast.88), calls=%async_computation.3 | async-start | bytes 524288 | tf_op jit(solution)/shard_map/all_to_all | solution.py:77
  129.9 6.7 %copy-start.5 = (f32[128,128]{1,0:T(8,128)}, f32[128,128]{1,0:T(8,128)S(1)}, u32[]{:S(2)}) copy-start(f32[128,128]{1,0:T(8,128)S(1)} %convert_reduce_fusion.1) | copy-start | bytes 196612
  130.7 0.5 copy-start.12
  133.1 9.8 %all-to-all-start.5 = ((bf16[8,2,512]{2,1,0:T(2,128)(2,1)}), bf16[8,2,512]{2,1,0:T(2,128)(2,1)S(1)}, u32[]{:S(2)}, u32[]{:S(2)}) async-start(bf16[8,2,512]{2,1,0:T(2,128)(2,1)} %reshape.262), calls=%async_computation.5 | async-start | bytes 32768 | tf_op jit(solution)/shard_map/all_to_all | solution.py:42
  142.9 1.6 copy-start.7
  144.5 4.5 %copy-start.11 = (f32[512]{0:T(512)S(1)}, f32[512]{0:T(512)}, u32[]{:S(2)}) copy-start(f32[512]{0:T(512)} %get-tuple-element.16) | copy-start | bytes 6148
  144.5 25.8 %all-to-all-start.4 = ((bf16[8,128,1024]{2,1,0:T(8,128)(2,1)}), bf16[8,128,1024]{2,1,0:T(8,128)(2,1)S(1)}, u32[]{:S(2)}, u32[]{:S(2)}) async-start(bf16[8,128,1024]{2,1,0:T(8,128)(2,1)} %broadcast_in_dim.33), calls=%async_computation.4 | async-start | bytes 4194304 | tf_op jit(solution)/shard_map/all_to_all | solution.py:42
  150.4 1.5 copy-start.6
  150.5 1.5 copy-start.16
  150.5 1.5 copy-start.19
  150.5 2.6 copy-start.8
  153.1 17.7 %copy-start.13 = (f32[128]{0:T(128)S(1)}, f32[128]{0:T(128)}, u32[]{:S(2)}) copy-start(f32[128]{0:T(128)} %copy-done.12) | copy-start | bytes 1540
  170.7 1.0 copy-start.4
  185.4 8.5 %all-to-all-start.10 = ((f32[2,32,8,1024]{3,2,1,0:T(8,128)}), f32[2,32,8,1024]{3,2,1,0:T(8,128)S(1)}, u32[]{:S(2)}, u32[]{:S(2)}) async-start(f32[2,32,8,1024]{3,2,1,0:T(8,128)} %bitcast.86), calls=%async_computation.10 | async-start | bytes 4194304 | tf_op jit(solution)/shard_map/all_to_all | solution.py:63
  193.9 39.0 %all-to-all-start.7 = ((f32[32,1,4114]{2,1,0:T(1,128)}), f32[32,1,4114]{2,1,0:T(1,128)}, u32[]{:S(2)}, u32[]{:S(2)}) async-start(f32[32,1,4114]{2,1,0:T(1,128)} %all_to_all.57), calls=%async_computation.7 | async-start | bytes 1081344 | tf_op jit(solution)/shard_map/all_to_all | solution.py:71
  232.9 57.3 %all-to-all-start.11 = ((f32[32,8,1024]{2,1,0:T(8,128)}), f32[32,8,1024]{2,1,0:T(8,128)S(1)}, u32[]{:S(2)}, u32[]{:S(2)}) async-start(f32[32,8,1024]{2,1,0:T(8,128)} %reduce_sum.110), calls=%async_computation.11 | async-start | bytes 2097152 | tf_op jit(solution)/shard_map/all_to_all | solution.py:71
  291.3 37.1 %all-to-all-start.8 = ((f32[32,1,4114]{2,1,0:T(1,128)}), f32[32,1,4114]{2,1,0:T(1,128)S(1)}, u32[]{:S(2)}, u32[]{:S(2)}) async-start(f32[32,1,4114]{2,1,0:T(1,128)} %broadcast_in_dim.35), calls=%async_computation.8 | async-start | bytes 1081344 | tf_op jit(solution)/shard_map/all_to_all | solution.py:42
where the time goes:
time: 345 us; the launch traced here: 343 us
  waiting for transfers between devices  170 us (49%)
  blocking collectives  89.1 us (26%)
  starting transfers between devices  41.5 us (12%)
  local copies, waits for them, and re-layouts  24.5 us (7%)
  other arithmetic  9.6 us (3%)
  matrix products  5.52 us (2%)
    all_to_all x2, waiting for transfers between devices, summed_rows(): lax.all_to_all(nearer, far, split_axis=0, concat_axis=0, tiled=True)  83.5 us
    all_to_all x4, waiting for transfers between devices, copy_for_each(): return lax.all_to_all(copies, axis, split_axis=0, concat_axis=0, tiled=True)  74.8 us
    all_to_all x1, blocking collectives, side_by_side(): lax.all_to_all(both, axis, split_axis=split_dim, concat_axis=concat_dim,...  40.1 us
    all_gather x1, blocking collectives, rows_first(): out = lax.all_gather(both, axis, axis=0, tiled=True)  29.2 us
    all_to_all x4, starting transfers between devices, copy_for_each(): return lax.all_to_all(copies, axis, split_axis=0, concat_axis=0, tiled=True)  17.4 us
    all_to_all x1, blocking collectives, sum_at_owner(): pieces = lax.all_to_all(cut_along(shard, dim, size), axis, 0, 0, tiled=True)  12.4 us
    all_to_all x2, waiting for transfers between devices, sent_and_summed(): lax.all_to_all(pieces, axis, split_axis=0, concat_axis=0, tiled=True)  11.7 us
    all_to_all x2, starting transfers between devices, summed_rows(): lax.all_to_all(nearer, far, split_axis=0, concat_axis=0, tiled=True)  10.2 us
  transfers between devices with their start and end apart: 9, of which 8 were waited for; matrix products, arithmetic and copies ran while one was open for 4% of the time, Pallas kernels for 0%

commit v1 on v0

v1 whole, which is shorter than its diff:
```python
import jax
import jax.numpy as jnp
from jax import lax
from jax.experimental import pallas as pl
from jax.experimental.pallas import tpu as pltpu
from jax.sharding import Mesh
from jax.sharding import PartitionSpec as P

MESH = pl.DeviceIdType.MESH
DP = ("z", "xl", "c")
MP = ("y", "xh")
ALL = DP + MP
BF = jnp.bfloat16
F32 = jnp.float32

R = 128
H = 1024
NZ = 16
NT = (((1,), (1,)), ((), ()))
TN = (((0,), (0,)), ((), ()))


def dot(a, b, dims=(((1,), (0,)), ((), ()))):
    return lax.dot_general(a, b, dims, preferred_element_type=F32)


def remote(src, dst, send, recv, to):
    return pltpu.make_async_remote_copy(
        src_ref=src, dst_ref=dst, send_sem=send, recv_sem=recv, device_id=to, device_id_type=MESH
    )


def each(n, body):
    def step(t, carry):
        body(t)
        return carry

    lax.fori_loop(0, n, step, 0)


def far_first(t):
    odd = t % 2
    return NZ // 2 + odd * ((t + 1) // 2) - (1 - odd) * (t // 2)


def kernel(
    x_ref,
    jac_ref,
    tgt_ref,
    w1_ref,
    b1_ref,
    hw_ref,
    hb_ref,
    dec_ref,
    fw_ref,
    fb_ref,
    hg_ref,
    hbg_ref,
    dg_ref,
    ft,
    tsend,
    tfull,
    dblk,
    dmat,
    jbuf,
    tbuf,
    pbuf,
    rbuf,
    gsend,
    grecv,
    gown,
    hsend,
    hrecv,
    qsend,
    qrecv,
    fsend,
    frecv,
    zsend,
    zrecv,
    zall,
    hall,
    fall,
    s_tan,
    r_tan,
    s_dec,
    r_dec,
    s_half,
    r_half,
    s_jac,
    r_jac,
    s_tgt,
    r_tgt,
    s_back,
    r_back,
    s_gc,
    r_gc,
    s_gz,
    r_gz,
    s_q,
    r_q,
    s_f,
    r_f,
    s_zr,
    r_zr,
    s_zg,
    r_zg,
    s_h,
    r_h,
    s_fa,
    r_fa,
):
    z, xl, c = lax.axis_index("z"), lax.axis_index("xl"), lax.axis_index("c")
    y, xh = lax.axis_index("y"), lax.axis_index("xh")
    m = y * 2 + xh
    q = m * 2 + xl
    e = c * 2 + xl
    w = m * 4 + e
    b = c * NZ + z

    def at_z(zz):
        return {"z": zz}

    def at_zc(bb):
        return {"z": bb % NZ, "c": bb // NZ}

    def at_q(qq):
        return {"y": qq // 4, "xh": (qq // 2) % 2, "xl": qq % 2}

    def at_e(ee):
        return {"c": ee // 2, "xl": ee % 2}

    def at_w(ww):
        return {"y": ww // 8, "xh": (ww // 4) % 2, "c": (ww // 2) % 2, "xl": ww % 2}

    partner = {"c": 1 - c}
    barrier = pltpu.get_barrier_semaphore()

    def greet_zc(t):
        pl.semaphore_signal(barrier, inc=1, device_id=at_zc((b + t + 1) % 32), device_id_type=MESH)

    def greet_w(t):
        pl.semaphore_signal(barrier, inc=1, device_id=at_w((w + t + 1) % 32), device_id_type=MESH)

    each(31, greet_zc)
    each(31, greet_w)

    w1 = w1_ref[...].astype(F32)
    x_row = jnp.broadcast_to(x_ref[...], (16, R))
    first_pre = dot(x_row.astype(BF), w1_ref[...]) + b1_ref[...].astype(F32)
    first_act = jnp.tanh(first_pre)[0:1]
    first_slope = 1.0 - first_act * first_act
    top16 = lax.broadcasted_iota(jnp.int32, (16, H), 0) == 0
    ft[0:R, :] = (first_slope * w1).astype(BF)
    ft[R : R + 16, :] = jnp.where(top16, jnp.broadcast_to(first_act, (16, H)), 0.0).astype(BF)
    lin = dot(ft[...], hw_ref[...])
    hidden_lin = lin[0:R]
    hidden_act = jnp.tanh(lin[R : R + 1] + hb_ref[...].astype(F32))
    hidden_slope = 1.0 - hidden_act * hidden_act
    top = lax.broadcasted_iota(jnp.int32, (16, R), 0) == 0
    tsend[0:R, :] = (hidden_slope * hidden_lin).astype(BF)
    tsend[R : R + 16, :] = jnp.where(top, jnp.broadcast_to(hidden_act, (16, R)), 0.0).astype(BF)
    tfull[:, R + 16 :, :] = jnp.zeros((2, 2 * R - R - 16, H), BF)
    mine = pl.ds(pl.multiple_of(m * R, R), R)
    tfull[xl, 0 : R + 16, mine] = tsend[...]
    dblk[c, z] = dec_ref[...]
    jbuf[b] = jac_ref[b]
    tbuf[b] = tgt_ref[b]

    pl.semaphore_wait(barrier, 62)

    def tan_copy(peer, src):
        lanes = pl.ds(pl.multiple_of((src // 2) * R, R), R)
        return remote(
            tsend, tfull.at[src % 2, pl.ds(0, R + 16), lanes], s_tan.at[peer], r_tan.at[src], at_q(peer)
        )

    def dec_copy(peer, src):
        return remote(dec_ref, dblk.at[c, src], s_dec.at[peer], r_dec.at[src], at_z(peer))

    def jac_copy(peer, src):
        return remote(jac_ref.at[peer], jbuf.at[src], s_jac.at[peer], r_jac.at[src], at_zc(peer))

    def tgt_copy(peer, src):
        return remote(tgt_ref.at[peer], tbuf.at[src], s_tgt.at[peer], r_tgt.at[src], at_zc(peer))

    def half_copy(side):
        return remote(dblk.at[side], dblk.at[side], s_half, r_half, partner)

    def others(n, me, copy, what):
        def go(t):
            peer = (me + t + 1) % n
            if what == "start":
                copy(peer, me).start()
            elif what == "recv":
                copy(me, peer).wait_recv()
            else:
                copy(peer, me).wait_send()

        each(n - 1, go)

    def start_z(copy):
        def go(t):
            copy((z + far_first(t)) % NZ, z).start()

        each(NZ - 1, go)

    others(16, q, tan_copy, "start")
    start_z(dec_copy)

    def start_jac(t):
        zz = (z + far_first(t)) % NZ
        for cc in range(2):
            peer = cc * NZ + zz
            jac_copy(peer, b).start()
            tgt_copy(peer, b).start()

    each(NZ - 1, start_jac)
    pb = (1 - c) * NZ + z
    jac_copy(pb, b).start()
    tgt_copy(pb, b).start()

    others(NZ, z, dec_copy, "recv")
    half_copy(c).start()
    own_half = dblk[c].astype(F32).reshape(R, H).astype(BF)
    dmat[pl.ds(pl.multiple_of(c * R, R), R), :] = own_half
    others(16, q, tan_copy, "recv")
    others(32, b, jac_copy, "recv")
    others(32, b, tgt_copy, "recv")
    half_copy(1 - c).wait_recv()
    other_half = dblk[1 - c].astype(F32).reshape(R, H).astype(BF)
    dmat[pl.ds(pl.multiple_of((1 - c) * R, R), R), :] = other_half

    lane = lax.broadcasted_iota(jnp.int32, (32, 8, R), 2)
    row = lax.broadcasted_iota(jnp.int32, (32, 8, R), 1)
    tgt = jnp.broadcast_to(tbuf[...], (32, 8, R))
    miss = []
    for i in range(2):
        want = jnp.sum(jnp.where(lane == row + 8 * i, tgt, 0.0), axis=2, keepdims=True)
        want = jnp.where(lane == 0, jnp.broadcast_to(want, (32, 8, R)), 0.0).reshape(2 * R, R)
        stored = jbuf[:, i].astype(F32).reshape(2 * R, R)
        net = dot(dmat[...], tfull[i], NT)
        miss_i = (net - jnp.concatenate([stored, want], axis=1)).astype(BF)
        miss.append(miss_i)
        pbuf[i] = dot(miss_i, dmat[...], TN)[0 : R + 16].astype(BF)

    def back_copy(peer, src):
        lanes = pl.ds(pl.multiple_of((peer // 2) * R, R), R)
        return remote(
            pbuf.at[peer % 2, :, lanes], rbuf.at[src], s_back.at[peer], r_back.at[src], at_q(peer)
        )

    others(16, q, back_copy, "start")

    gown[...] = dot(miss[0], tfull[0]) + dot(miss[1], tfull[1])
    theirs = gown[pl.ds(pl.multiple_of((1 - c) * R, R), R), :]
    gsend[...] = theirs.reshape(NZ, 8, H).astype(BF)

    def gc_copy():
        return remote(gsend, grecv, s_gc, r_gc, partner)

    gc_copy().start()
    ours = gown[pl.ds(pl.multiple_of(c * R, R), R), :].reshape(NZ, 8, H)
    gc_copy().wait_recv()
    hsend[...] = (ours + grecv[...].astype(F32)).astype(BF)

    def gz_copy(peer, src):
        return remote(hsend.at[peer], hrecv.at[src], s_gz.at[peer], r_gz.at[src], at_z(peer))

    start_z(gz_copy)
    hrecv[z] = hsend[z]

    others(16, q, back_copy, "recv")
    rbuf[q] = pbuf[xl, :, mine]
    back = jnp.sum(rbuf[...].astype(F32), axis=0)
    tan_back = back[0:R]
    act_back = back[R : R + 1]
    lin_round = (tan_back * hidden_slope).astype(BF)
    pre_back = act_back * hidden_slope - 2.0 * hidden_act * hidden_slope * jnp.sum(
        tan_back * hidden_lin, axis=0, keepdims=True
    )
    pre_round = jnp.where(top, jnp.broadcast_to(pre_back, (16, R)), 0.0).astype(BF)
    both = jnp.concatenate([lin_round, pre_round], axis=0)
    qsend[...] = dot(ft[...], both, TN).astype(BF).reshape(4, 2 * R, R)

    def q_copy(peer, src):
        return remote(qsend.at[peer], qrecv.at[src], s_q.at[peer], r_q.at[src], at_e(peer))

    others(4, e, q_copy, "start")
    qrecv[e] = qsend[e]

    low = dot(both, hw_ref[...], NT)
    tan_lower = low[0:R]
    pre_lower = low[R : R + 1] * first_slope - 2.0 * first_act * first_slope * jnp.sum(
        tan_lower * w1, axis=0, keepdims=True
    )
    x_col = jnp.transpose(jnp.broadcast_to(x_ref[...], (R, R)))[:, 0:1]
    fw = x_col * pre_lower + tan_lower * first_slope
    place = lax.broadcasted_iota(jnp.int32, (16, H), 1) // R == m
    second = lax.broadcasted_iota(jnp.int32, (16, H), 0) == 1
    pre_wide = jnp.concatenate([pre_back] * 8, axis=1)
    tail = jnp.where(top16, jnp.broadcast_to(pre_lower, (16, H)), 0.0)
    tail = tail + jnp.where(second & place, jnp.broadcast_to(pre_wide, (16, H)), 0.0)
    for k in range(4):
        fsend[k, 0:32, :] = fw[32 * k : 32 * k + 32].astype(BF)
        fsend[k, 32:48, :] = tail.astype(BF)

    def f_copy(peer, src):
        lanes = pl.ds(pl.multiple_of((peer // 4) * R, R), R)
        return remote(
            fsend.at[peer % 4, :, lanes], frecv.at[src], s_f.at[peer], r_f.at[src], at_w(peer)
        )

    others(32, w, f_copy, "start")
    frecv[w] = fsend[e, :, mine]

    others(4, e, q_copy, "recv")
    quarter = jnp.sum(qrecv[...].astype(F32), axis=0)
    zsend[:, 0:2] = quarter.reshape(NZ, 2, 8, R).astype(BF)
    zsend[:, 2:3] = jnp.zeros((NZ, 1, 8, R), BF)
    others(32, w, f_copy, "recv")
    piece = jnp.sum(frecv[...].astype(F32), axis=0)
    zsend[0:6, 2] = piece.reshape(6, 8, R).astype(BF)

    def zr_copy(peer, src):
        return remote(zsend.at[peer], zrecv.at[src], s_zr.at[peer], r_zr.at[src], at_z(peer))

    start_z(zr_copy)
    zrecv[z] = zsend[z]
    others(NZ, z, zr_copy, "recv")
    zall[z] = jnp.sum(zrecv[...].astype(F32), axis=0).astype(BF)

    def zg_copy(peer, src):
        return remote(zall.at[src], zall.at[src], s_zg.at[peer], r_zg.at[src], at_z(peer))

    start_z(zg_copy)

    others(NZ, z, gz_copy, "recv")
    dg_ref[...] = jnp.sum(hrecv[...].astype(F32), axis=0)

    others(NZ, z, zg_copy, "recv")

    def h_copy(peer, src):
        return remote(zall.at[:, pl.ds(0, 2)], hall.at[src], s_h.at[peer], r_h.at[src], at_e(peer))

    def fa_copy(peer, src):
        return remote(
            zall.at[pl.ds(0, 6), 2], fall.at[src], s_fa.at[peer], r_fa.at[src], at_w(peer)
        )

    others(32, w, fa_copy, "start")
    others(4, e, h_copy, "start")
    hall[e] = zall[:, 0:2]
    fall[w] = zall[0:6, 2]
    hbg_ref[...] = zall[4, 2].astype(F32)[1:2]
    others(4, e, h_copy, "recv")
    hg_ref[...] = hall[...].astype(F32).reshape(H, R)
    others(32, w, fa_copy, "recv")
    for mm in range(8):
        for ee in range(4):
            got = fall[4 * mm + ee].astype(F32)
            fw_ref[32 * ee : 32 * ee + 32, R * mm : R * mm + R] = got[0:4].reshape(32, R)
            if ee == 0:
                fb_ref[:, R * mm : R * mm + R] = got[4, 0:1]

    half_copy(c).wait_send()
    gc_copy().wait_send()
    others(16, q, tan_copy, "send")
    others(NZ, z, dec_copy, "send")
    others(32, b, jac_copy, "send")
    others(32, b, tgt_copy, "send")
    others(16, q, back_copy, "send")
    others(NZ, z, gz_copy, "send")
    others(4, e, q_copy, "send")
    others(32, w, f_copy, "send")
    others(NZ, z, zr_copy, "send")
    others(NZ, z, zg_copy, "send")
    others(4, e, h_copy, "send")
    others(32, w, fa_copy, "send")


def on_device(inputs_store, window, targets_store, jac_store, first_weight, first_bias, hidden_weight, hidden_bias, decoder_weight):
    sample = lax.axis_index("z") * 4 + lax.axis_index("c") * 2 + lax.axis_index("xl")
    x = inputs_store[lax.dynamic_slice_in_dim(window, sample, 1)].astype(F32)
    order = window.reshape(NZ, 2, 2).transpose(1, 0, 2).reshape(64)
    jac = jac_store[order].reshape(32, 2, 8, R)
    tgt = targets_store[order].astype(F32).reshape(32, 1, 16)
    tgt = jnp.pad(tgt, ((0, 0), (0, 0), (0, R - 16)))
    vmem = pl.BlockSpec(memory_space=pltpu.VMEM)
    dma = pltpu.SemaphoreType.DMA
    fw, fb, hg, hbg, dg = pl.pallas_call(
        kernel,
        out_shape=(
            jax.ShapeDtypeStruct((R, H), F32),
            jax.ShapeDtypeStruct((1, H), F32),
            jax.ShapeDtypeStruct((H, R), F32),
            jax.ShapeDtypeStruct((1, R), F32),
            jax.ShapeDtypeStruct((8, H), F32),
        ),
        in_specs=[vmem] * 8,
        out_specs=(vmem,) * 5,
        scratch_shapes=[
            pltpu.VMEM((R + 16, H), BF),
            pltpu.VMEM((R + 16, R), BF),
            pltpu.VMEM((2, 2 * R, H), BF),
            pltpu.VMEM((2, NZ, 8, H), BF),
            pltpu.VMEM((2 * R, H), BF),
            pltpu.VMEM((32, 2, 8, R), BF),
            pltpu.VMEM((32, 1, R), F32),
            pltpu.VMEM((2, R + 16, H), BF),
            pltpu.VMEM((16, R + 16, R), BF),
            pltpu.VMEM((NZ, 8, H), BF),
            pltpu.VMEM((NZ, 8, H), BF),
            pltpu.VMEM((2 * R, H), F32),
            pltpu.VMEM((NZ, 8, H), BF),
            pltpu.VMEM((NZ, 8, H), BF),
            pltpu.VMEM((4, 2 * R, R), BF),
            pltpu.VMEM((4, 2 * R, R), BF),
            pltpu.VMEM((4, 48, H), BF),
            pltpu.VMEM((32, 48, R), BF),
            pltpu.VMEM((NZ, 3, 8, R), BF),
            pltpu.VMEM((NZ, 3, 8, R), BF),
            pltpu.VMEM((NZ, 3, 8, R), BF),
            pltpu.VMEM((4, NZ, 2, 8, R), BF),
            pltpu.VMEM((32, 6, 8, R), BF),
            dma((16,)), dma((16,)),
            dma((NZ,)), dma((NZ,)),
            dma, dma,
            dma((32,)), dma((32,)),
            dma((32,)), dma((32,)),
            dma((16,)), dma((16,)),
            dma, dma,
            dma((NZ,)), dma((NZ,)),
            dma((4,)), dma((4,)),
            dma((32,)), dma((32,)),
            dma((NZ,)), dma((NZ,)),
            dma((NZ,)), dma((NZ,)),
            dma((4,)), dma((4,)),
            dma((32,)), dma((32,)),
        ],
        compiler_params=pltpu.CompilerParams(
            collective_id=0, has_side_effects=True, vmem_limit_bytes=40 * 1024 * 1024
        ),
    )(x, jac, tgt, first_weight, first_bias.reshape(1, H), hidden_weight, hidden_bias.reshape(1, R), decoder_weight)
    return fw, fb.reshape(H), hg, hbg.reshape(R), dg


def solution(mesh):
    torus = Mesh(mesh.devices.reshape(NZ, 2, 2, 4, 2), ALL)
    return jax.shard_map(
        on_device,
        mesh=torus,
        in_specs=(P(), P(), P(None, ALL), P(None, ALL, None), P(), P(), P(None, MP), P(MP), P(ALL, None)),
        out_specs=(P(), P(), P(None, MP), P(MP), P(ALL, None)),
        check_vma=False,
    )
```

time: 345 us -> 102 us (0.30)
  waiting for transfers between devices: 170 us -> 0 us
  Pallas kernels: 0 us -> 91 us
  blocking collectives: 89.1 us -> 0 us
  starting transfers between devices: 41.5 us -> 0 us
  local copies, waits for them, and re-layouts: 24.5 us -> 7.07 us
  other arithmetic: 9.6 us -> 0.73 us
  matrix products: 5.52 us -> 0 us
    all_to_all x9 -> x0, waiting for transfers between devices: 170 us -> none  [the longest x2 83.5 us: summed_rows(): lax.all_to_all(nearer, far, split_axis=0, concat_axis=0, tiled=True)]
    pallas_call x0 -> x1, Pallas kernels: none -> 91 us  [on_device(): pl.pallas_call(kernel, out_shape=(jax.ShapeDtypeStruct((R, H), F32), jax....]
    all_to_all x3 -> x0, blocking collectives: 60 us -> none  [the longest x1 40.1 us: side_by_side(): lax.all_to_all(both, axis, split_axis=split_dim, concat_axis=concat_dim,...]
    all_to_all x9 -> x0, starting transfers between devices: 41.5 us -> none  [the longest x4 17.4 us: copy_for_each(): return lax.all_to_all(copies, axis, split_axis=0, concat_axis=0, tiled=True)]
    all_gather x1 -> x0, blocking collectives: 29.2 us -> none  [rows_first(): out = lax.all_gather(both, axis, axis=0, tiled=True)]
    reduce_sum x9 -> x0, other arithmetic: 5.89 us -> none  [the longest x2 3.38 us: sum_at_owner(): return jnp.sum(pieces, axis=0)]
    dot_general x11 -> x0, matrix products: 5.52 us -> none  [the longest x1 1.42 us: on_device(): jnp.einsum('hzy,hym->zm', jacobian_residual, tangent_full_rows, preferred...]
    slice x6 -> x0, local copies, waits for them, and re-layouts: 4.87 us -> none  [the longest x5 4.86 us: together(): subtotal[b:e].reshape(a.shape)]
  transfers between devices with their start and end apart: 9 -> 0, of which waited for: 8 -> 0; matrix products, arithmetic and copies ran while one was open for 4% -> 0% of each run, Pallas kernels for 0% -> 0%
where the time goes in v1:
time: 102 us
  Pallas kernels  91 us (89%)
  local copies, waits for them, and re-layouts  7.07 us (7%)
  between operations  2.73 us (3%)
    pallas_call x1, Pallas kernels, on_device(): pl.pallas_call(kernel, out_shape=(jax.ShapeDtypeStruct((R, H), F32), jax....  91 us
    unnamed x22, local copies, waits for them, and re-layouts  4.9 us

profile of v1, /device:TPU:1, one launch (start us, length us, event | category | flops | bytes accessed | tf_op | source)
XLA Modules:
  0.0 101.5 jit_solution(16456232283392244754)
XLA Ops:
  0.6 0.0 copy-start
  0.7 0.0 copy-start.7
  0.7 0.7 copy-done.7
  1.4 0.6 dynamic_slice.3
  3.9 0.0 copy-start.6
  3.9 0.7 dynamic-slice_convert_fusion.x_ref
  4.6 0.0 copy-done.6
  4.6 0.1 reshape.80
  4.8 0.1 reshape.81
  4.9 0.0 copy-start.5
  4.9 0.0 copy-done
  4.9 0.0 copy-start.1
  4.9 0.0 copy-start.2
  4.9 0.6 gather_fusion
  5.6 0.0 copy-done.5
  5.6 0.2 copy.17
  5.8 0.6 gather_fusion.1
  6.4 0.1 convert_element_type.18
  6.5 0.0 copy-start.3
  6.5 0.0 copy-start.4
  6.5 0.0 copy-done.1
  6.5 0.0 copy-done.2
  6.6 0.7 copy-done.3
  7.2 0.0 copy-done.4
  7.2 91.0 %shard_map.128 = (f32[128,1024]{1,0:T(8,128)S(1)}, f32[1,1024]{1,0:T(1,128)S(1)}, f32[1024,128]{1,0:T(8,128)S(1)}, f32[1,128]{1,0:T(1,128)S(1)}, f32[8,1024]{1,0:T(8,128)S(1)}) custom-call(f32[1,128]{1,0:T(1,128)S(1)} %dynamic-slice_convert_fusion.x_ref, bf16[32,2,8,128]{3,2,1,0:T(8,128)(2,1)S(1)} %bitcast.8, f32[32,1,128]{2,1,0:T(1,128)S(1)} %pad_convert_fusion.tgt_ref, ...), custom_call_target="tpu_custom_call" | custom-call | tf_op jit(solution)/shard_map/pallas_call | solution.py:390
  98.2 0.8 copy.24
  99.0 0.6 copy.25
  99.6 0.8 copy.26
  100.4 0.5 copy.27
  100.9 0.6 copy.28
  (5 shorter events, 0.0 us)
Async XLA Ops:
  0.6 4.3 %copy-start = (bf16[512,8,128]{2,1,0:T(8,128)(2,1)S(1)}, bf16[512,8,128]{2,1,0:T(8,128)(2,1)}, u32[]{:S(2)}) copy-start(bf16[512,8,128]{2,1,0:T(8,128)(2,1)} %param.12) | copy-start | bytes 3145732
  0.7 0.7 copy-start.7
  3.9 0.7 copy-start.6
  4.9 0.7 copy-start.5
  4.9 1.6 %copy-start.1 = (bf16[128,1024]{1,0:T(8,128)(2,1)S(1)}, bf16[128,1024]{1,0:T(8,128)(2,1)}, u32[]{:S(2)}) copy-start(bf16[128,1024]{1,0:T(8,128)(2,1)} %w1_ref.1) | copy-start | bytes 786436
  4.9 1.6 %copy-start.2 = (bf16[1024,128]{1,0:T(8,128)(2,1)S(1)}, bf16[1024,128]{1,0:T(8,128)(2,1)}, u32[]{:S(2)}) copy-start(bf16[1024,128]{1,0:T(8,128)(2,1)} %hw_ref.1) | copy-start | bytes 786436
  6.5 0.7 copy-start.3
  6.5 0.7 copy-start.4

commit v2 on v1

v2 whole, which is shorter than its diff:
```python
import jax
import jax.numpy as jnp
from jax import lax
from jax.experimental import pallas as pl
from jax.experimental.pallas import tpu as pltpu
from jax.sharding import Mesh
from jax.sharding import PartitionSpec as P

MESH = pl.DeviceIdType.MESH
DP = ("z", "xl", "c")
MP = ("y", "xh")
ALL = DP + MP
BF = jnp.bfloat16
F32 = jnp.float32

R = 128
H = 1024
NZ = 16
WIDE = H + R
NT = (((1,), (1,)), ((), ()))
TN = (((0,), (0,)), ((), ()))


def dot(a, b, dims=(((1,), (0,)), ((), ()))):
    return lax.dot_general(a, b, dims, preferred_element_type=F32)


def remote(src, dst, send, recv, to):
    return pltpu.make_async_remote_copy(
        src_ref=src, dst_ref=dst, send_sem=send, recv_sem=recv, device_id=to, device_id_type=MESH
    )


def each(n, body):
    def step(t, carry):
        body(t)
        return carry

    lax.fori_loop(0, n, step, 0)


def far_first(t):
    odd = t % 2
    return NZ // 2 + odd * ((t + 1) // 2) - (1 - odd) * (t // 2)


def slot_of(zz):
    return (zz % 4) * 4 + zz // 4


def kernel(
    ids_ref,
    idv_ref,
    xs_ref,
    jac_ref,
    tgt_ref,
    w1_ref,
    b1_ref,
    hw_ref,
    hb_ref,
    dec_ref,
    fw_ref,
    fb_ref,
    hg_ref,
    hbg_ref,
    dg_ref,
    ft,
    tsend,
    tfull,
    dsend,
    dblk,
    dmat,
    jsend,
    jbuf,
    pbuf,
    rbuf,
    gsend,
    grecv,
    gown,
    hsend,
    hrecv,
    qsend,
    qrecv,
    fsend,
    frecv,
    zsend,
    zrecv,
    zall,
    ysend,
    yrecv,
    yall,
    hall,
    fall,
    sent,
    came,
):
    z, xl, c = lax.axis_index("z"), lax.axis_index("xl"), lax.axis_index("c")
    y, xh = lax.axis_index("y"), lax.axis_index("xh")
    m = y * 2 + xh
    q = m * 2 + xl
    e = c * 2 + xl
    w = m * 4 + e
    zs = slot_of(z)
    b = c * NZ + zs

    def at_z(zz):
        return {"z": zz}

    def at_zc(bb):
        return {"z": bb % NZ, "c": bb // NZ}

    def at_q(qq):
        return {"y": qq // 4, "xh": (qq // 2) % 2, "xl": qq % 2}

    def at_e(ee):
        return {"c": ee // 2, "xl": ee % 2}

    def at_w(ww):
        return {"y": ww // 8, "xh": (ww // 4) % 2, "c": (ww // 2) % 2, "xl": ww % 2}

    partner = {"c": 1 - c}
    barrier = pltpu.get_barrier_semaphore()

    def greet_z(t):
        zz = (z + far_first(t)) % NZ
        for cc in range(2):
            pl.semaphore_signal(barrier, inc=1, device_id={"z": zz, "c": cc}, device_id_type=MESH)

    def greet_w(t):
        pl.semaphore_signal(barrier, inc=1, device_id=at_w((w + t + 1) % 32), device_id_type=MESH)

    each(NZ - 1, greet_z)
    each(31, greet_w)

    def pick(zz):
        for cc in range(2):
            for i in range(2):
                jsend[cc * NZ + slot_of(zz), i] = jac_ref[ids_ref[zz * 4 + cc * 2 + i]]

    each(NZ, pick)
    hot = (lax.broadcasted_iota(jnp.int32, (512, 64), 0) == idv_ref[...]).astype(F32).astype(BF)
    dsend[:, 0:H] = dec_ref[...]
    dsend[:, H : H + 64] = dot(tgt_ref[...], hot).astype(BF)
    dsend[:, H + 64 :] = jnp.zeros((8, R - 64), BF)
    own = ids_ref[z * 4 + c * 2 + xl]
    x_hot = (lax.broadcasted_iota(jnp.int32, (16, 512), 1) == own).astype(F32).astype(BF)
    x_rows = dot(x_hot, xs_ref[...])

    w1 = w1_ref[...].astype(F32)
    first_pre = dot(x_rows.astype(BF), w1_ref[...]) + b1_ref[...].astype(F32)
    first_act = jnp.tanh(first_pre)[0:1]
    first_slope = 1.0 - first_act * first_act
    top16 = lax.broadcasted_iota(jnp.int32, (16, H), 0) == 0
    ft[0:R, :] = (first_slope * w1).astype(BF)
    ft[R : R + 16, :] = jnp.where(top16, jnp.broadcast_to(first_act, (16, H)), 0.0).astype(BF)
    lin = dot(ft[...], hw_ref[...])
    hidden_lin = lin[0:R]
    hidden_act = jnp.tanh(lin[R : R + 1] + hb_ref[...].astype(F32))
    hidden_slope = 1.0 - hidden_act * hidden_act
    top = lax.broadcasted_iota(jnp.int32, (16, R), 0) == 0
    tsend[0:R, :] = (hidden_slope * hidden_lin).astype(BF)
    tsend[R : R + 16, :] = jnp.where(top, jnp.broadcast_to(hidden_act, (16, R)), 0.0).astype(BF)
    tfull[:, R + 16 :, :] = jnp.zeros((2, 2 * R - R - 16, H), BF)
    mine = pl.ds(pl.multiple_of(m * R, R), R)
    tfull[xl, 0 : R + 16, mine] = tsend[...]
    dblk[c, zs] = dsend[...]
    jbuf[b] = jsend[b]

    with jax.named_scope("barrier"):
        pl.semaphore_wait(barrier, 61)

    def tan_copy(peer, src):
        lanes = pl.ds(pl.multiple_of((src // 2) * R, R), R)
        dst = tfull.at[src % 2, pl.ds(0, R + 16), lanes]
        return remote(tsend, dst, sent.at[0], came.at[0], at_q(peer))

    def far_copy(peer, src):
        return remote(dsend, dblk.at[c, slot_of(src)], sent.at[1], came.at[1], at_z(peer))

    def near_copy(peer, first, count):
        part = dblk.at[c, pl.ds(first, count)]
        return remote(part, part, sent.at[2], came.at[2], at_z(peer))

    def half_copy(side):
        return remote(dblk.at[side], dblk.at[side], sent.at[3], came.at[3], partner)

    def jac_copy(zz, cc):
        return remote(
            jsend.at[cc * NZ + slot_of(zz)], jbuf.at[b], sent.at[4], came.at[4], {"z": zz, "c": cc}
        )

    def start(n, me, copy):
        with jax.named_scope(copy.__name__ + "_start"):
            each(n - 1, lambda t: copy((me + t + 1) % n, me).start())

    def start_z(copy):
        with jax.named_scope(copy.__name__ + "_start"):
            each(NZ - 1, lambda t: copy((z + far_first(t)) % NZ, z).start())

    def recv(k, ref):
        with jax.named_scope(f"recv{k}"):
            remote(ref, ref, sent.at[k], came.at[k], partner).wait_recv()

    def left(k, ref):
        remote(ref, ref, sent.at[k], came.at[k], partner).wait_send()

    for d in (8, 4, 12):
        far_copy((z + d) % NZ, z).start()
    start(16, q, tan_copy)

    def start_jac(t):
        zz = (z + far_first(t)) % NZ
        for cc in range(2):
            jac_copy(zz, cc).start()

    each(NZ - 1, start_jac)
    jac_copy(z, 1 - c).start()

    recv(1, dblk.at[0, pl.ds(0, 3)])
    group = (z % 4) * 4
    part = group + 2 * ((z // 4) % 2)
    near_copy((z + 2) % NZ, part, 2).start()
    near_copy((z + 14) % NZ, part, 2).start()
    near_copy((z + 1) % NZ, group, 4).start()
    near_copy((z + 15) % NZ, group, 4).start()
    recv(2, dblk.at[0, pl.ds(0, 12)])
    half_copy(c).start()

    def unpack(side):
        rows = pl.ds(pl.multiple_of(side * R, R), R)
        dmat[rows, :] = dblk[side].astype(F32).reshape(R, WIDE).astype(BF)

    unpack(c)
    recv(0, rbuf.at[pl.ds(0, 15)])
    recv(4, jbuf.at[pl.ds(0, 31)])
    recv(3, dblk.at[0])
    unpack(1 - c)

    lane = lax.broadcasted_iota(jnp.int32, (2 * R, R), 1)
    tgt = dmat[:, H:].astype(F32)
    dec = dmat[:, 0:H]
    miss = []
    for i in range(2):
        want = jnp.sum(jnp.where(lane == z * 4 + c * 2 + i, tgt, 0.0), axis=1, keepdims=True)
        want = jnp.where(lane == 0, jnp.broadcast_to(want, (2 * R, R)), 0.0)
        stored = jbuf[:, i].astype(F32).reshape(2 * R, R)
        net = dot(dec, tfull[i], NT)
        miss_i = (net - jnp.concatenate([stored, want], axis=1)).astype(BF)
        miss.append(miss_i)
        pbuf[i] = dot(miss_i, dec, TN)[0 : R + 16].astype(BF)

    def back_copy(peer, src):
        lanes = pl.ds(pl.multiple_of((peer // 2) * R, R), R)
        return remote(
            pbuf.at[peer % 2, :, lanes], rbuf.at[src], sent.at[5], came.at[5], at_q(peer)
        )

    start(16, q, back_copy)

    gown[...] = dot(miss[0], tfull[0]) + dot(miss[1], tfull[1])
    theirs = gown[pl.ds(pl.multiple_of((1 - c) * R, R), R), :]
    gsend[...] = theirs.reshape(NZ, 8, H).astype(BF)
    remote(gsend, grecv, sent.at[6], came.at[6], partner).start()
    ours = gown[pl.ds(pl.multiple_of(c * R, R), R), :].reshape(NZ, 8, H)
    recv(6, grecv)
    hsend[...] = (ours + grecv[...].astype(F32)).astype(BF)

    def gz_copy(peer, src):
        return remote(
            hsend.at[slot_of(peer)], hrecv.at[slot_of(src)], sent.at[7], came.at[7], at_z(peer)
        )

    start_z(gz_copy)
    hrecv[zs] = hsend[zs]

    recv(5, rbuf.at[pl.ds(0, 15)])
    rbuf[q] = pbuf[xl, :, mine]
    back = jnp.sum(rbuf[...].astype(F32), axis=0)
    tan_back = back[0:R]
    act_back = back[R : R + 1]
    lin_round = (tan_back * hidden_slope).astype(BF)
    pre_back = act_back * hidden_slope - 2.0 * hidden_act * hidden_slope * jnp.sum(
        tan_back * hidden_lin, axis=0, keepdims=True
    )
    pre_round = jnp.where(top, jnp.broadcast_to(pre_back, (16, R)), 0.0).astype(BF)
    both = jnp.concatenate([lin_round, pre_round], axis=0)
    qsend[...] = dot(ft[...], both, TN).astype(BF).reshape(4, 2 * R, R)

    def q_copy(peer, src):
        return remote(qsend.at[peer], qrecv.at[src], sent.at[8], came.at[8], at_e(peer))

    start(4, e, q_copy)
    qrecv[e] = qsend[e]

    low = dot(both, hw_ref[...], NT)
    tan_lower = low[0:R]
    pre_lower = low[R : R + 1] * first_slope - 2.0 * first_act * first_slope * jnp.sum(
        tan_lower * w1, axis=0, keepdims=True
    )
    x_col = jnp.transpose(jnp.broadcast_to(x_rows[0:1], (R, R)))[:, 0:1]
    fw = x_col * pre_lower + tan_lower * first_slope
    place = lax.broadcasted_iota(jnp.int32, (8, H), 1) // R == m
    line = lax.broadcasted_iota(jnp.int32, (8, H), 0)
    pre_wide = jnp.concatenate([pre_back] * 8, axis=1)
    tail = jnp.where(line == 0, jnp.broadcast_to(pre_lower, (8, H)), 0.0)
    tail = tail + jnp.where((line == 1) & place, jnp.broadcast_to(pre_wide, (8, H)), 0.0)
    for k in range(4):
        fsend[k, 0:4] = fw[32 * k : 32 * k + 32].reshape(4, 8, H).astype(BF)
        fsend[k, 4] = tail.astype(BF)

    def f_copy(peer, src):
        lanes = pl.ds(pl.multiple_of((peer // 4) * R, R), R)
        return remote(
            fsend.at[peer % 4, :, :, lanes], frecv.at[src], sent.at[9], came.at[9], at_w(peer)
        )

    start(32, w, f_copy)
    frecv[w] = fsend[e, :, :, mine]

    recv(8, qrecv.at[pl.ds(0, 3)])
    quarter = jnp.sum(qrecv[...].astype(F32), axis=0)
    zsend[...] = quarter.reshape(NZ, 2, 8, R).astype(BF)

    def zr_copy(peer, src):
        return remote(zsend.at[peer], zrecv.at[src], sent.at[10], came.at[10], at_z(peer))

    start_z(zr_copy)
    zrecv[z] = zsend[z]

    recv(9, frecv.at[pl.ds(0, 31)])
    ysend[...] = jnp.sum(frecv[...].astype(F32), axis=0).astype(BF)
    for t in range(5):

        @pl.when(z != t)
        def _():
            remote(ysend.at[t], yrecv.at[z], sent.at[11], came.at[11], at_z(t)).start()

        @pl.when(z == t)
        def _():
            yrecv[z] = ysend[t]

    recv(10, zrecv.at[pl.ds(0, 15)])
    zall[z] = jnp.sum(zrecv[...].astype(F32), axis=0).astype(BF)

    def zg_copy(peer, src):
        return remote(zall.at[src], zall.at[src], sent.at[12], came.at[12], at_z(peer))

    start_z(zg_copy)

    def y_copy(peer, src):
        return remote(yall.at[src], yall.at[src], sent.at[13], came.at[13], at_z(peer))

    @pl.when(z < 5)
    def _():
        recv(11, yrecv.at[pl.ds(0, 15)])
        yall[z] = jnp.sum(yrecv[...].astype(F32), axis=0).astype(BF)
        start_z(y_copy)

    recv(7, hrecv.at[pl.ds(0, 15)])
    dg_ref[...] = jnp.sum(hrecv[...].astype(F32), axis=0)

    recv(12, zall.at[pl.ds(0, 15)])

    def h_copy(peer, src):
        return remote(zall, hall.at[src], sent.at[14], came.at[14], at_e(peer))

    start(4, e, h_copy)

    @pl.when(z < 5)
    def _():
        recv(13, yall.at[pl.ds(0, 4)])

    @pl.when(z >= 5)
    def _():
        recv(13, yall.at[pl.ds(0, 5)])

    def fa_copy(peer, src):
        return remote(yall.at[pl.ds(0, 5)], fall.at[src], sent.at[15], came.at[15], at_w(peer))

    start(32, w, fa_copy)
    hall[e] = zall[...]
    fall[w] = yall[0:5]
    hbg_ref[...] = yall[4].astype(F32)[1:2]
    recv(14, hall.at[pl.ds(0, 3)])
    hg_ref[...] = hall[...].astype(F32).reshape(H, R)
    recv(15, fall.at[pl.ds(0, 31)])
    for mm in range(8):
        for ee in range(4):
            got = fall[4 * mm + ee].astype(F32)
            fw_ref[32 * ee : 32 * ee + 32, R * mm : R * mm + R] = got[0:4].reshape(32, R)
            if ee == 0:
                fb_ref[:, R * mm : R * mm + R] = got[4, 0:1]

    left(0, rbuf.at[pl.ds(0, 15)])
    left(1, dblk.at[0, pl.ds(0, 3)])
    left(2, dblk.at[0, pl.ds(0, 12)])
    left(3, dblk.at[0])
    left(4, jbuf.at[pl.ds(0, 31)])
    left(5, rbuf.at[pl.ds(0, 15)])
    left(6, grecv)
    left(7, hrecv.at[pl.ds(0, 15)])
    left(8, qrecv.at[pl.ds(0, 3)])
    left(9, frecv.at[pl.ds(0, 31)])
    left(10, zrecv.at[pl.ds(0, 15)])

    @pl.when(z < 5)
    def _():
        left(11, yall.at[pl.ds(0, 4)])
        left(13, yrecv.at[pl.ds(0, 15)])

    @pl.when(z >= 5)
    def _():
        left(11, yall.at[pl.ds(0, 5)])

    left(12, zrecv.at[pl.ds(0, 15)])
    left(14, hall.at[pl.ds(0, 3)])
    left(15, fall.at[pl.ds(0, 31)])


def on_device(
    inputs_store,
    window,
    targets_store,
    jac_store,
    first_weight,
    first_bias,
    hidden_weight,
    hidden_bias,
    decoder_weight,
):
    vmem = pl.BlockSpec(memory_space=pltpu.VMEM)
    smem = pl.BlockSpec(memory_space=pltpu.SMEM)
    dma = pltpu.SemaphoreType.DMA
    fw, fb, hg, hbg, dg = pl.pallas_call(
        kernel,
        out_shape=(
            jax.ShapeDtypeStruct((R, H), F32),
            jax.ShapeDtypeStruct((1, H), F32),
            jax.ShapeDtypeStruct((H, R), F32),
            jax.ShapeDtypeStruct((1, R), F32),
            jax.ShapeDtypeStruct((8, H), F32),
        ),
        in_specs=[smem] + [vmem] * 9,
        out_specs=(vmem,) * 5,
        scratch_shapes=[
            pltpu.VMEM((R + 16, H), BF),
            pltpu.VMEM((R + 16, R), BF),
            pltpu.VMEM((2, 2 * R, H), BF),
            pltpu.VMEM((8, WIDE), BF),
            pltpu.VMEM((2, NZ, 8, WIDE), BF),
            pltpu.VMEM((2 * R, WIDE), BF),
            pltpu.VMEM((32, 2, 8, R), BF),
            pltpu.VMEM((32, 2, 8, R), BF),
            pltpu.VMEM((2, R + 16, H), BF),
            pltpu.VMEM((16, R + 16, R), BF),
            pltpu.VMEM((NZ, 8, H), BF),
            pltpu.VMEM((NZ, 8, H), BF),
            pltpu.VMEM((2 * R, H), F32),
            pltpu.VMEM((NZ, 8, H), BF),
            pltpu.VMEM((NZ, 8, H), BF),
            pltpu.VMEM((4, 2 * R, R), BF),
            pltpu.VMEM((4, 2 * R, R), BF),
            pltpu.VMEM((4, 5, 8, H), BF),
            pltpu.VMEM((32, 5, 8, R), BF),
            pltpu.VMEM((NZ, 2, 8, R), BF),
            pltpu.VMEM((NZ, 2, 8, R), BF),
            pltpu.VMEM((NZ, 2, 8, R), BF),
            pltpu.VMEM((5, 8, R), BF),
            pltpu.VMEM((NZ, 8, R), BF),
            pltpu.VMEM((NZ, 8, R), BF),
            pltpu.VMEM((4, NZ, 2, 8, R), BF),
            pltpu.VMEM((32, 5, 8, R), BF),
            dma((16,)),
            dma((16,)),
        ],
        compiler_params=pltpu.CompilerParams(
            collective_id=0, has_side_effects=True, vmem_limit_bytes=40 * 1024 * 1024
        ),
    )(
        window,
        window.reshape(1, 64),
        inputs_store,
        jac_store,
        targets_store.T,
        first_weight,
        first_bias.reshape(1, H),
        hidden_weight,
        hidden_bias.reshape(1, R),
        decoder_weight,
    )
    return fw, fb.reshape(H), hg, hbg.reshape(R), dg


def solution(mesh):
    torus = Mesh(mesh.devices.reshape(NZ, 2, 2, 4, 2), ALL)
    return jax.shard_map(
        on_device,
        mesh=torus,
        in_specs=(
            P(),
            P(),
            P(None, ALL),
            P(None, ALL, None),
            P(),
            P(),
            P(None, MP),
            P(MP),
            P(ALL, None),
        ),
        out_specs=(P(), P(), P(None, MP), P(MP), P(ALL, None)),
        check_vma=False,
    )
```

time: 102 us -> 83.5 us (0.82)
  Pallas kernels: 91 us -> 73.7 us
  between operations: 2.73 us -> 0.69 us
  local copies, waits for them, and re-layouts: 7.07 us -> 8.76 us
    pallas_call x1, Pallas kernels: 91 us -> 73.7 us  [on_device(): pl.pallas_call(kernel, out_shape=(jax.ShapeDtypeStruct((R, H), F32), jax....]
    unnamed x22 -> x21, local copies, waits for them, and re-layouts: 4.9 us -> 8.06 us
    gather x2 -> x0, local copies, waits for them, and re-layouts: 1.27 us -> none  [the longest x1 0.64 us: on_device(): tgt = targets_store[order].astype(F32).reshape(32, 1, 16)]
where the time goes in v2:
time: 83.5 us; the launch traced here: 83.1 us
  Pallas kernels  73.7 us (88%)
  local copies, waits for them, and re-layouts  8.76 us (10%)
    pallas_call x1, Pallas kernels, on_device(): pl.pallas_call(kernel, out_shape=(jax.ShapeDtypeStruct((R, H), F32), jax....  73.7 us
    unnamed x21, local copies, waits for them, and re-layouts  8.06 us

profile of v2, /device:TPU:1, one launch (start us, length us, event | category | flops | bytes accessed | tf_op | source)
XLA Modules:
  0.0 83.1 jit_solution(2257912611125425942)
XLA Ops:
  0.6 0.0 copy-start.5
  0.6 0.0 copy-start.6
  0.7 0.0 copy-start.7
  0.7 0.7 reshape.26.b1_ref
  1.4 0.0 copy-done.5
  1.4 0.0 copy-done.6
  1.4 0.0 copy-done.7
  1.4 0.0 copy-start
  1.4 1.2 %copy-done = bf16[512,8,128]{2,1,0:T(8,128)(2,1)S(1)} copy-done((bf16[512,8,128]{2,1,0:T(8,128)(2,1)S(1)}, bf16[512,8,128]{2,1,0:T(8,128)(2,1)}, u32[]{:S(2)}) %copy-start) | copy-done | bytes 1048600
  2.6 0.0 copy-start.1
  2.6 0.9 %copy-done.1 = bf16[128,1024]{1,0:T(8,128)(2,1)S(1)} copy-done((bf16[128,1024]{1,0:T(8,128)(2,1)S(1)}, bf16[128,1024]{1,0:T(8,128)(2,1)}, u32[]{:S(2)}) %copy-start.1) | copy-done | bytes 262168
  3.6 0.0 copy-start.2
  3.6 0.9 %copy-done.2 = bf16[1024,128]{1,0:T(8,128)(2,1)S(1)} copy-done((bf16[1024,128]{1,0:T(8,128)(2,1)S(1)}, bf16[1024,128]{1,0:T(8,128)(2,1)}, u32[]{:S(2)}) %copy-start.2) | copy-done | bytes 262168
  4.5 0.0 copy-start.3
  4.5 0.9 %copy-done.3 = bf16[512,128]{1,0:T(8,128)(2,1)S(1)} copy-done((bf16[512,128]{1,0:T(8,128)(2,1)S(1)}, bf16[512,128]{1,0:T(8,128)(2,1)}, u32[]{:S(2)}) %copy-start.3) | copy-done | bytes 131096
  5.4 0.0 copy-start.4
  5.4 0.7 copy-done.4
  6.1 73.7 %shard_map.128 = (f32[128,1024]{1,0:T(8,128)S(1)}, f32[1,1024]{1,0:T(1,128)S(1)}, f32[1024,128]{1,0:T(8,128)S(1)}, f32[1,128]{1,0:T(1,128)S(1)}, f32[8,1024]{1,0:T(8,128)S(1)}) custom-call(s32[64]{0:T(128)S(1)} %copy-done.6, s32[1,64]{1,0:T(1,128)S(1)} %bitcast.7, bf16[512,128]{1,0:T(8,128)(2,1)S(1)} %copy-done.3, bf16[512,8,128]{2,1,0:T(8,128)(2,1)S(1)} %copy-done, ...), custom_call_target="tpu_custom_call" | custom-call | tf_op jit(solution)/shard_map/pallas_call | solution.py:434
  79.8 0.8 copy.19
  80.6 0.6 copy.20
  81.2 0.8 copy.21
  82.0 0.5 copy.22
  82.5 0.6 copy.23
Async XLA Ops:
  0.6 0.7 copy-start.5
  0.6 0.7 copy-start.6
  0.7 0.7 copy-start.7
  1.4 1.2 %copy-start = (bf16[512,8,128]{2,1,0:T(8,128)(2,1)S(1)}, bf16[512,8,128]{2,1,0:T(8,128)(2,1)}, u32[]{:S(2)}) copy-start(bf16[512,8,128]{2,1,0:T(8,128)(2,1)} %jac_ref.1) | copy-start | bytes 3145732
  2.6 0.9 %copy-start.1 = (bf16[128,1024]{1,0:T(8,128)(2,1)S(1)}, bf16[128,1024]{1,0:T(8,128)(2,1)}, u32[]{:S(2)}) copy-start(bf16[128,1024]{1,0:T(8,128)(2,1)} %w1_ref.1) | copy-start | bytes 786436
  3.6 0.9 %copy-start.2 = (bf16[1024,128]{1,0:T(8,128)(2,1)S(1)}, bf16[1024,128]{1,0:T(8,128)(2,1)}, u32[]{:S(2)}) copy-start(bf16[1024,128]{1,0:T(8,128)(2,1)} %hw_ref.1) | copy-start | bytes 786436
  4.5 0.9 %copy-start.3 = (bf16[512,128]{1,0:T(8,128)(2,1)S(1)}, bf16[512,128]{1,0:T(8,128)(2,1)}, u32[]{:S(2)}) copy-start(bf16[512,128]{1,0:T(8,128)(2,1)} %xs_ref.1) | copy-start | bytes 393220
  5.4 0.7 copy-start.4

commit v3 on v2

--- a/solution.py
+++ b/solution.py
@@ -17,6 +17,7 @@
 H = 1024
 NZ = 16
 WIDE = H + R
+VMEM_MOST = 67043328
 NT = (((1,), (1,)), ((), ()))
 TN = (((0,), (0,)), ((), ()))
 
@@ -44,13 +45,21 @@
     return NZ // 2 + odd * ((t + 1) // 2) - (1 - odd) * (t // 2)
 
 
-def slot_of(zz):
-    return (zz % 4) * 4 + zz // 4
-
-
 def kernel(
     ids_ref,
     idv_ref,
+    xs_hbm,
+    jac_hbm,
+    tgt_hbm,
+    w1_hbm,
+    b1_hbm,
+    hw_hbm,
+    hb_hbm,
+    dec_hbm,
+    hall_hbm,
+    fall_hbm,
+    tile_hbm,
+    dg_hbm,
     xs_ref,
     jac_ref,
     tgt_ref,
@@ -59,11 +68,6 @@
     hw_ref,
     hb_ref,
     dec_ref,
-    fw_ref,
-    fb_ref,
-    hg_ref,
-    hbg_ref,
-    dg_ref,
     ft,
     tsend,
     tfull,
@@ -91,8 +95,12 @@
     yall,
     hall,
     fall,
+    tile,
+    dg_ref,
     sent,
     came,
+    taken,
+    put,
 ):
     z, xl, c = lax.axis_index("z"), lax.axis_index("xl"), lax.axis_index("c")
     y, xh = lax.axis_index("y"), lax.axis_index("xh")
@@ -100,8 +108,7 @@
     q = m * 2 + xl
     e = c * 2 + xl
     w = m * 4 + e
-    zs = slot_of(z)
-    b = c * NZ + zs
+    b = c * NZ + z
 
     def at_z(zz):
         return {"z": zz}
@@ -129,25 +136,99 @@
     def greet_w(t):
         pl.semaphore_signal(barrier, inc=1, device_id=at_w((w + t + 1) % 32), device_id_type=MESH)
 
+    homes = (
+        (jac_hbm, jac_ref),
+        (tgt_hbm, tgt_ref),
+        (dec_hbm, dec_ref),
+        (xs_hbm, xs_ref),
+        (w1_hbm, w1_ref),
+        (hw_hbm, hw_ref),
+        (b1_hbm, b1_ref),
+        (hb_hbm, hb_ref),
+    )
+    loads = [pltpu.make_async_copy(a, v, taken.at[k]) for k, (a, v) in enumerate(homes)]
+    for load in loads:
+        load.start()
     each(NZ - 1, greet_z)
     each(31, greet_w)
+
+    tfull[:, R + 16 :, :] = jnp.zeros((2, 2 * R - R - 16, H), BF)
+    hot = (lax.broadcasted_iota(jnp.int32, (512, 64), 0) == idv_ref[...]).astype(F32).astype(BF)
+    for load in loads[0:3]:
+        load.wait()
 
     def pick(zz):
         for cc in range(2):
             for i in range(2):
-                jsend[cc * NZ + slot_of(zz), i] = jac_ref[ids_ref[zz * 4 + cc * 2 + i]]
+                jsend[cc * NZ + zz, i] = jac_ref[ids_ref[zz * 4 + cc * 2 + i]]
 
     each(NZ, pick)
-    hot = (lax.broadcasted_iota(jnp.int32, (512, 64), 0) == idv_ref[...]).astype(F32).astype(BF)
     dsend[:, 0:H] = dec_ref[...]
     dsend[:, H : H + 64] = dot(tgt_ref[...], hot).astype(BF)
     dsend[:, H + 64 :] = jnp.zeros((8, R - 64), BF)
+    dblk[c, z] = dsend[...]
+    jbuf[b] = jsend[b]
+    for load in loads[3:]:
+        load.wait()
+
+    with jax.named_scope("barrier"):
+        pl.semaphore_wait(barrier, 61)
+
+    def tan_copy(peer, src):
+        lanes = pl.ds(pl.multiple_of((src // 2) * R, R), R)
+        dst = tfull.at[src % 2, pl.ds(0, R + 16), lanes]
+        return remote(tsend, dst, sent.at[0], came.at[0], at_q(peer))
+
+    def own_copy(d, k):
+        return remote(
+            dsend, dblk.at[c, z], sent.at[k], came.at[k], {"z": (z + d) % NZ}
+        )
+
+    def pass_copy(block, d):
+        part = dblk.at[c, (z + block) % NZ]
+        return remote(part, part, sent.at[2], came.at[2], {"z": (z + d) % NZ})
+
+    def half_copy(side):
+        return remote(dblk.at[side], dblk.at[side], sent.at[3], came.at[3], partner)
+
+    def jac_copy(zz, cc):
+        return remote(
+            jsend.at[cc * NZ + zz], jbuf.at[b], sent.at[4], came.at[4], {"z": zz, "c": cc}
+        )
+
+    def start(n, me, copy):
+        with jax.named_scope(copy.__name__ + "_start"):
+            each(n - 1, lambda t: copy((me + t + 1) % n, me).start())
+
+    def start_z(copy):
+        with jax.named_scope(copy.__name__ + "_start"):
+            each(NZ - 1, lambda t: copy((z + far_first(t)) % NZ, z).start())
+
+    def recv(k, ref):
+        with jax.named_scope(f"recv{k}"):
+            remote(ref, ref, sent.at[k], came.at[k], partner).wait_recv()
+
+    def left(k, ref):
+        remote(ref, ref, sent.at[k], came.at[k], partner).wait_send()
+
+    def start_jac(t):
+        zz = (z + far_first(t)) % NZ
+        for cc in range(2):
+            jac_copy(zz, cc).start()
+
+    for d in (5, 11):
+        own_copy(d, 1).start()
+    for d in (1, 15, 2, 14):
+        own_copy(d, 16).start()
+    each(5, start_jac)
+
     own = ids_ref[z * 4 + c * 2 + xl]
     x_hot = (lax.broadcasted_iota(jnp.int32, (16, 512), 1) == own).astype(F32).astype(BF)
     x_rows = dot(x_hot, xs_ref[...])
-
     w1 = w1_ref[...].astype(F32)
-    first_pre = dot(x_rows.astype(BF), w1_ref[...]) + b1_ref[...].astype(F32)
+    b1 = b1_ref[...].astype(F32)
+    b1 = jnp.concatenate([b1[k : k + 1] for k in range(8)], axis=1)
+    first_pre = dot(x_rows.astype(BF), w1_ref[...]) + b1
     first_act = jnp.tanh(first_pre)[0:1]
     first_slope = 1.0 - first_act * first_act
     top16 = lax.broadcasted_iota(jnp.int32, (16, H), 0) == 0
@@ -160,70 +241,20 @@
     top = lax.broadcasted_iota(jnp.int32, (16, R), 0) == 0
     tsend[0:R, :] = (hidden_slope * hidden_lin).astype(BF)
     tsend[R : R + 16, :] = jnp.where(top, jnp.broadcast_to(hidden_act, (16, R)), 0.0).astype(BF)
-    tfull[:, R + 16 :, :] = jnp.zeros((2, 2 * R - R - 16, H), BF)
+    start(16, q, tan_copy)
     mine = pl.ds(pl.multiple_of(m * R, R), R)
     tfull[xl, 0 : R + 16, mine] = tsend[...]
-    dblk[c, zs] = dsend[...]
-    jbuf[b] = jsend[b]
-
-    with jax.named_scope("barrier"):
-        pl.semaphore_wait(barrier, 61)
-
-    def tan_copy(peer, src):
-        lanes = pl.ds(pl.multiple_of((src // 2) * R, R), R)
-        dst = tfull.at[src % 2, pl.ds(0, R + 16), lanes]
-        return remote(tsend, dst, sent.at[0], came.at[0], at_q(peer))
-
-    def far_copy(peer, src):
-        return remote(dsend, dblk.at[c, slot_of(src)], sent.at[1], came.at[1], at_z(peer))
-
-    def near_copy(peer, first, count):
-        part = dblk.at[c, pl.ds(first, count)]
-        return remote(part, part, sent.at[2], came.at[2], at_z(peer))
-
-    def half_copy(side):
-        return remote(dblk.at[side], dblk.at[side], sent.at[3], came.at[3], partner)
-
-    def jac_copy(zz, cc):
-        return remote(
-            jsend.at[cc * NZ + slot_of(zz)], jbuf.at[b], sent.at[4], came.at[4], {"z": zz, "c": cc}
-        )
-
-    def start(n, me, copy):
-        with jax.named_scope(copy.__name__ + "_start"):
-            each(n - 1, lambda t: copy((me + t + 1) % n, me).start())
-
-    def start_z(copy):
-        with jax.named_scope(copy.__name__ + "_start"):
-            each(NZ - 1, lambda t: copy((z + far_first(t)) % NZ, z).start())
-
-    def recv(k, ref):
-        with jax.named_scope(f"recv{k}"):
-            remote(ref, ref, sent.at[k], came.at[k], partner).wait_recv()
-
-    def left(k, ref):
-        remote(ref, ref, sent.at[k], came.at[k], partner).wait_send()
-
-    for d in (8, 4, 12):
-        far_copy((z + d) % NZ, z).start()
-    start(16, q, tan_copy)
-
-    def start_jac(t):
-        zz = (z + far_first(t)) % NZ
-        for cc in range(2):
-            jac_copy(zz, cc).start()
-
-    each(NZ - 1, start_jac)
+
+    recv(1, dblk.at[0, pl.ds(0, 2)])
+    for d in (2, 14, 1, 15):
+        for block in (5, 11):
+            pass_copy(block, d).start()
+    side = 1 - 2 * (z % 2)
+    pass_copy(NZ - 5 * side, NZ + 3 * side).start()
+    each(10, lambda t: start_jac(t + 5))
     jac_copy(z, 1 - c).start()
-
-    recv(1, dblk.at[0, pl.ds(0, 3)])
-    group = (z % 4) * 4
-    part = group + 2 * ((z // 4) % 2)
-    near_copy((z + 2) % NZ, part, 2).start()
-    near_copy((z + 14) % NZ, part, 2).start()
-    near_copy((z + 1) % NZ, group, 4).start()
-    near_copy((z + 15) % NZ, group, 4).start()
-    recv(2, dblk.at[0, pl.ds(0, 12)])
+    recv(16, dblk.at[0, pl.ds(0, 4)])
+    recv(2, dblk.at[0, pl.ds(0, 9)])
     half_copy(c).start()
 
     def unpack(side):
@@ -267,11 +298,11 @@
 
     def gz_copy(peer, src):
         return remote(
-            hsend.at[slot_of(peer)], hrecv.at[slot_of(src)], sent.at[7], came.at[7], at_z(peer)
+            hsend.at[peer], hrecv.at[src], sent.at[7], came.at[7], at_z(peer)
         )
 
     start_z(gz_copy)
-    hrecv[zs] = hsend[zs]
+    hrecv[z] = hsend[z]
 
     recv(5, rbuf.at[pl.ds(0, 15)])
     rbuf[q] = pbuf[xl, :, mine]
@@ -284,14 +315,6 @@
     )
     pre_round = jnp.where(top, jnp.broadcast_to(pre_back, (16, R)), 0.0).astype(BF)
     both = jnp.concatenate([lin_round, pre_round], axis=0)
-    qsend[...] = dot(ft[...], both, TN).astype(BF).reshape(4, 2 * R, R)
-
-    def q_copy(peer, src):
-        return remote(qsend.at[peer], qrecv.at[src], sent.at[8], came.at[8], at_e(peer))
-
-    start(4, e, q_copy)
-    qrecv[e] = qsend[e]
-
     low = dot(both, hw_ref[...], NT)
     tan_lower = low[0:R]
     pre_lower = low[R : R + 1] * first_slope - 2.0 * first_act * first_slope * jnp.sum(
@@ -317,6 +340,26 @@
     start(32, w, f_copy)
     frecv[w] = fsend[e, :, :, mine]
 
+    qsend[...] = dot(ft[...], both, TN).astype(BF).reshape(4, 2 * R, R)
+
+    def q_copy(peer, src):
+        return remote(qsend.at[peer], qrecv.at[src], sent.at[8], came.at[8], at_e(peer))
+
+    start(4, e, q_copy)
+    qrecv[e] = qsend[e]
+
+    recv(9, frecv.at[pl.ds(0, 31)])
+    ysend[...] = jnp.sum(frecv[...].astype(F32), axis=0).astype(BF)
+    for t in range(5):
+
+        @pl.when(z != t)
+        def _():
+            remote(ysend.at[t], yrecv.at[z], sent.at[11], came.at[11], at_z(t)).start()
+
+        @pl.when(z == t)
+        def _():
+            yrecv[z] = ysend[t]
+
     recv(8, qrecv.at[pl.ds(0, 3)])
     quarter = jnp.sum(qrecv[...].astype(F32), axis=0)
     zsend[...] = quarter.reshape(NZ, 2, 8, R).astype(BF)
@@ -326,26 +369,6 @@
 
     start_z(zr_copy)
     zrecv[z] = zsend[z]
-
-    recv(9, frecv.at[pl.ds(0, 31)])
-    ysend[...] = jnp.sum(frecv[...].astype(F32), axis=0).astype(BF)
-    for t in range(5):
-
-        @pl.when(z != t)
-        def _():
-            remote(ysend.at[t], yrecv.at[z], sent.at[11], came.at[11], at_z(t)).start()
-
-        @pl.when(z == t)
-        def _():
-            yrecv[z] = ysend[t]
-
-    recv(10, zrecv.at[pl.ds(0, 15)])
-    zall[z] = jnp.sum(zrecv[...].astype(F32), axis=0).astype(BF)
-
-    def zg_copy(peer, src):
-        return remote(zall.at[src], zall.at[src], sent.at[12], came.at[12], at_z(peer))
-
-    start_z(zg_copy)
 
     def y_copy(peer, src):
         return remote(yall.at[src], yall.at[src], sent.at[13], came.at[13], at_z(peer))
@@ -356,15 +379,23 @@
         yall[z] = jnp.sum(yrecv[...].astype(F32), axis=0).astype(BF)
         start_z(y_copy)
 
+    recv(10, zrecv.at[pl.ds(0, 15)])
+    zall[z] = jnp.sum(zrecv[...].astype(F32), axis=0).astype(BF)
+
+    def zg_copy(peer, src):
+        return remote(zall.at[src], zall.at[src], sent.at[12], came.at[12], at_z(peer))
+
+    start_z(zg_copy)
+
     recv(7, hrecv.at[pl.ds(0, 15)])
     dg_ref[...] = jnp.sum(hrecv[...].astype(F32), axis=0)
-
-    recv(12, zall.at[pl.ds(0, 15)])
-
-    def h_copy(peer, src):
-        return remote(zall, hall.at[src], sent.at[14], came.at[14], at_e(peer))
-
-    start(4, e, h_copy)
+    outs = (
+        pltpu.make_async_copy(dg_ref, dg_hbm, put.at[0]),
+        pltpu.make_async_copy(tile, tile_hbm, put.at[1]),
+        pltpu.make_async_copy(hall, hall_hbm, put.at[2]),
+        pltpu.make_async_copy(fall, fall_hbm, put.at[3]),
+    )
+    outs[0].start()
 
     @pl.when(z < 5)
     def _():
@@ -378,22 +409,26 @@
         return remote(yall.at[pl.ds(0, 5)], fall.at[src], sent.at[15], came.at[15], at_w(peer))
 
     start(32, w, fa_copy)
+
+    recv(12, zall.at[pl.ds(0, 15)])
+
+    def h_copy(peer, src):
+        return remote(zall, hall.at[src], sent.at[14], came.at[14], at_e(peer))
+
+    start(4, e, h_copy)
     hall[e] = zall[...]
     fall[w] = yall[0:5]
-    hbg_ref[...] = yall[4].astype(F32)[1:2]
+    tile[...] = yall[4]
+    outs[1].start()
     recv(14, hall.at[pl.ds(0, 3)])
-    hg_ref[...] = hall[...].astype(F32).reshape(H, R)
+    outs[2].start()
     recv(15, fall.at[pl.ds(0, 31)])
-    for mm in range(8):
-        for ee in range(4):
-            got = fall[4 * mm + ee].astype(F32)
-            fw_ref[32 * ee : 32 * ee + 32, R * mm : R * mm + R] = got[0:4].reshape(32, R)
-            if ee == 0:
-                fb_ref[:, R * mm : R * mm + R] = got[4, 0:1]
+    outs[3].start()
 
     left(0, rbuf.at[pl.ds(0, 15)])
-    left(1, dblk.at[0, pl.ds(0, 3)])
-    left(2, dblk.at[0, pl.ds(0, 12)])
+    left(1, dblk.at[0, pl.ds(0, 2)])
+    left(16, dblk.at[0, pl.ds(0, 4)])
+    left(2, dblk.at[0, pl.ds(0, 9)])
     left(3, dblk.at[0])
     left(4, jbuf.at[pl.ds(0, 31)])
     left(5, rbuf.at[pl.ds(0, 15)])
@@ -415,6 +450,65 @@
     left(12, zrecv.at[pl.ds(0, 15)])
     left(14, hall.at[pl.ds(0, 3)])
     left(15, fall.at[pl.ds(0, 31)])
+    for out in outs:
+        out.wait()
+
+
+def unfold(
+    hall_hbm,
+    fall_hbm,
+    tile_hbm,
+    dg_hbm,
+    fw_hbm,
+    fb_hbm,
+    hg_hbm,
+    hb_hbm,
+    dgo_hbm,
+    hall,
+    fall,
+    tile,
+    dg,
+    fw,
+    fb,
+    hg,
+    hb,
+    got,
+    put,
+):
+    ins = (
+        pltpu.make_async_copy(hall_hbm, hall, got.at[0]),
+        pltpu.make_async_copy(fall_hbm, fall, got.at[1]),
+        pltpu.make_async_copy(dg_hbm, dg, got.at[2]),
+        pltpu.make_async_copy(tile_hbm, tile, got.at[3]),
+    )
+    outs = (
+        pltpu.make_async_copy(hg, hg_hbm, put.at[0]),
+        pltpu.make_async_copy(fw, fw_hbm, put.at[1]),
+        pltpu.make_async_copy(dg, dgo_hbm, put.at[2]),
+        pltpu.make_async_copy(hb, hb_hbm, put.at[3]),
+        pltpu.make_async_copy(fb, fb_hbm, put.at[4]),
+    )
+    for copy in ins:
+        copy.start()
+    ins[0].wait()
+    hg[...] = hall[...].astype(F32).reshape(H, R)
+    outs[0].start()
+    ins[1].wait()
+    for mm in range(8):
+        for ee in range(4):
+            piece = fall[4 * mm + ee].astype(F32)
+            fw[32 * ee : 32 * ee + 32, R * mm : R * mm + R] = piece[0:4].reshape(32, R)
+            if ee == 0:
+                fb[mm : mm + 1, :] = piece[4, 0:1]
+    outs[1].start()
+    outs[4].start()
+    ins[2].wait()
+    outs[2].start()
+    ins[3].wait()
+    hb[...] = tile[...].astype(F32)[1:2]
+    outs[3].start()
+    for copy in outs:
+        copy.wait()
 
 
 def on_device(
@@ -430,19 +524,27 @@
 ):
     vmem = pl.BlockSpec(memory_space=pltpu.VMEM)
     smem = pl.BlockSpec(memory_space=pltpu.SMEM)
+    hbm = pl.BlockSpec(memory_space=pltpu.HBM)
     dma = pltpu.SemaphoreType.DMA
-    fw, fb, hg, hbg, dg = pl.pallas_call(
+    hall = jax.ShapeDtypeStruct((4, NZ, 2, 8, R), BF)
+    fall = jax.ShapeDtypeStruct((32, 5, 8, R), BF)
+    tile = jax.ShapeDtypeStruct((8, R), BF)
+    dg = jax.ShapeDtypeStruct((8, H), F32)
+    raw = (hall, fall, tile, dg)
+    parts = pl.pallas_call(
         kernel,
-        out_shape=(
-            jax.ShapeDtypeStruct((R, H), F32),
-            jax.ShapeDtypeStruct((1, H), F32),
-            jax.ShapeDtypeStruct((H, R), F32),
-            jax.ShapeDtypeStruct((1, R), F32),
-            jax.ShapeDtypeStruct((8, H), F32),
-        ),
-        in_specs=[smem] + [vmem] * 9,
-        out_specs=(vmem,) * 5,
+        out_shape=raw,
+        in_specs=[smem, vmem] + [hbm] * 8,
+        out_specs=(hbm,) * 4,
         scratch_shapes=[
+            pltpu.VMEM((512, R), BF),
+            pltpu.VMEM((512, 8, R), BF),
+            pltpu.VMEM((8, 512), BF),
+            pltpu.VMEM((R, H), BF),
+            pltpu.VMEM((8, R), BF),
+            pltpu.VMEM((H, R), BF),
+            pltpu.VMEM((1, R), BF),
+            pltpu.VMEM((8, H), BF),
             pltpu.VMEM((R + 16, H), BF),
             pltpu.VMEM((R + 16, R), BF),
             pltpu.VMEM((2, 2 * R, H), BF),
@@ -470,11 +572,15 @@
             pltpu.VMEM((NZ, 8, R), BF),
             pltpu.VMEM((4, NZ, 2, 8, R), BF),
             pltpu.VMEM((32, 5, 8, R), BF),
-            dma((16,)),
-            dma((16,)),
+            pltpu.VMEM((8, R), BF),
+            pltpu.VMEM((8, H), F32),
+            dma((17,)),
+            dma((17,)),
+            dma((8,)),
+            dma((4,)),
         ],
         compiler_params=pltpu.CompilerParams(
-            collective_id=0, has_side_effects=True, vmem_limit_bytes=40 * 1024 * 1024
+            collective_id=0, has_side_effects=True, vmem_limit_bytes=VMEM_MOST
         ),
     )(
         window,
@@ -483,12 +589,28 @@
         jac_store,
         targets_store.T,
         first_weight,
-        first_bias.reshape(1, H),
+        first_bias.reshape(8, R),
         hidden_weight,
         hidden_bias.reshape(1, R),
         decoder_weight,
     )
-    return fw, fb.reshape(H), hg, hbg.reshape(R), dg
+    final = (
+        jax.ShapeDtypeStruct((R, H), F32),
+        jax.ShapeDtypeStruct((8, R), F32),
+        jax.ShapeDtypeStruct((H, R), F32),
+        jax.ShapeDtypeStruct((1, R), F32),
+        dg,
+    )
+    fw, fb, hg, hb, dgo = pl.pallas_call(
+        unfold,
+        out_shape=final,
+        in_specs=[hbm] * 4,
+        out_specs=(hbm,) * 5,
+        scratch_shapes=[pltpu.VMEM(a.shape, a.dtype) for a in raw + final[0:4]]
+        + [dma((4,)), dma((5,))],
+        compiler_params=pltpu.CompilerParams(vmem_limit_bytes=VMEM_MOST),
+    )(*parts)
+    return fw, fb.reshape(H), hg, hb.reshape(R), dgo
 
 
 def solution(mesh):

time: 83.5 us -> 74.6 us (0.89)
  local copies, waits for them, and re-layouts: 8.76 us -> 0 us
    unnamed x21 -> x0, local copies, waits for them, and re-layouts: 8.06 us -> none
    pallas_call x1 -> x2, Pallas kernels: 73.7 us -> 73.8 us  [the longest x1 71.8 us: on_device(): pl.pallas_call(kernel, out_shape=raw, in_specs=[smem, vmem] + [hbm] * 8,...]
where the time goes in v3:
time: 74.6 us; the launch traced here: 74.5 us
  Pallas kernels  73.8 us (99%)
    pallas_call x1, Pallas kernels, on_device(): pl.pallas_call(kernel, out_shape=raw, in_specs=[smem, vmem] + [hbm] * 8,...  71.8 us
    pallas_call x1, Pallas kernels, on_device(): pl.pallas_call(unfold, out_shape=final, in_specs=[hbm] * 4, out_specs=(hb...  2.04 us

profile of v3, /device:TPU:1, one launch (start us, length us, event | category | flops | bytes accessed | tf_op | source)
XLA Modules:
  0.0 74.5 jit_solution(14867710378297496488)
XLA Ops:
  0.6 71.8 %shard_map.128 = (bf16[4,16,2,8,128]{4,3,2,1,0:T(8,128)(2,1)}, bf16[32,5,8,128]{3,2,1,0:T(8,128)(2,1)}, bf16[8,128]{1,0:T(8,128)(2,1)}, f32[8,1024]{1,0:T(8,128)}) custom-call(s32[64]{0:T(128)} %ids_ref.1, s32[1,64]{1,0:T(1,128)} %bitcast.8, bf16[512,128]{1,0:T(8,128)(2,1)} %xs_hbm.1, bf16[512,8,128]{2,1,0:T(8,128)(2,1)} %jac_hbm.1, bf16[8,512]{1,0:T(8,128)(2,1)} %bitcast.6, ...), custom_call_target="tpu_custom_call" | custom-call | tf_op jit(solution)/shard_map/pallas_call | solution.py:534
  72.4 2.0 %shard_map.129 = (f32[128,1024]{1,0:T(8,128)}, f32[8,128]{1,0:T(8,128)}, f32[1024,128]{1,0:T(8,128)}, f32[1,128]{1,0:T(1,128)}, f32[8,1024]{1,0:T(8,128)}) custom-call(bf16[4,16,2,8,128]{4,3,2,1,0:T(8,128)(2,1)} %get-tuple-element.14.hall_hbm, bf16[32,5,8,128]{3,2,1,0:T(8,128)(2,1)} %get-tuple-element.15.fall_hbm, ...), custom_call_target="tpu_custom_call" | custom-call | tf_op jit(solution)/shard_map/pallas_call | solution.py:604

commit v4 on v3

--- a/solution.py
+++ b/solution.py
@@ -40,9 +40,21 @@
     lax.fori_loop(0, n, step, 0)
 
 
-def far_first(t):
-    odd = t % 2
-    return NZ // 2 + odd * ((t + 1) // 2) - (1 - odd) * (t // 2)
+def wrap(v, n):
+    return jnp.where(v >= n, v - n, v)
+
+
+FAR_FIRST = (8, 7, 9, 6, 10, 5, 11, 4, 12, 3, 13, 2, 14, 1, 15)
+PLANE = sorted(
+    (
+        (dy, dh, dl)
+        for dy in range(4)
+        for dh in range(2)
+        for dl in range(2)
+        if dy + dh + dl > 0
+    ),
+    key=lambda d: -(min(d[0], 4 - d[0]) + (2 if d[1:] == (1, 0) else max(d[1:]))),
+)
 
 
 def kernel(
@@ -76,6 +88,8 @@
     dmat,
     jsend,
     jbuf,
+    net,
+    tbytes,
     pbuf,
     rbuf,
     gsend,
@@ -84,8 +98,12 @@
     hsend,
     hrecv,
     qsend,
+    qpart,
+    qsum,
     qrecv,
     fsend,
+    fpart,
+    fsum,
     frecv,
     zsend,
     zrecv,
@@ -106,35 +124,17 @@
     y, xh = lax.axis_index("y"), lax.axis_index("xh")
     m = y * 2 + xh
     q = m * 2 + xl
-    e = c * 2 + xl
-    w = m * 4 + e
     b = c * NZ + z
 
-    def at_z(zz):
-        return {"z": zz}
-
-    def at_zc(bb):
-        return {"z": bb % NZ, "c": bb // NZ}
-
-    def at_q(qq):
-        return {"y": qq // 4, "xh": (qq // 2) % 2, "xl": qq % 2}
-
-    def at_e(ee):
-        return {"c": ee // 2, "xl": ee % 2}
-
-    def at_w(ww):
-        return {"y": ww // 8, "xh": (ww // 4) % 2, "c": (ww // 2) % 2, "xl": ww % 2}
+    def plane(d):
+        dy, dh, dl = d
+        yy = wrap(y + dy, 4)
+        hh = 1 - xh if dh else xh
+        ll = 1 - xl if dl else xl
+        return (yy * 2 + hh) * 2 + ll, {"y": yy, "xh": hh, "xl": ll}
 
     partner = {"c": 1 - c}
     barrier = pltpu.get_barrier_semaphore()
-
-    def greet_z(t):
-        zz = (z + far_first(t)) % NZ
-        for cc in range(2):
-            pl.semaphore_signal(barrier, inc=1, device_id={"z": zz, "c": cc}, device_id_type=MESH)
-
-    def greet_w(t):
-        pl.semaphore_signal(barrier, inc=1, device_id=at_w((w + t + 1) % 32), device_id_type=MESH)
 
     homes = (
         (jac_hbm, jac_ref),
@@ -149,8 +149,15 @@
     loads = [pltpu.make_async_copy(a, v, taken.at[k]) for k, (a, v) in enumerate(homes)]
     for load in loads:
         load.start()
-    each(NZ - 1, greet_z)
-    each(31, greet_w)
+    def greet(to):
+        pl.semaphore_signal(barrier, inc=1, device_id=to, device_id_type=MESH)
+
+    for d in FAR_FIRST:
+        for cc in range(2):
+            greet({"z": wrap(z + d, NZ), "c": cc})
+    for d in PLANE:
+        greet(plane(d)[1])
+    greet(partner)
 
     tfull[:, R + 16 :, :] = jnp.zeros((2, 2 * R - R - 16, H), BF)
     hot = (lax.broadcasted_iota(jnp.int32, (512, 64), 0) == idv_ref[...]).astype(F32).astype(BF)
@@ -172,21 +179,23 @@
         load.wait()
 
     with jax.named_scope("barrier"):
-        pl.semaphore_wait(barrier, 61)
-
-    def tan_copy(peer, src):
-        lanes = pl.ds(pl.multiple_of((src // 2) * R, R), R)
-        dst = tfull.at[src % 2, pl.ds(0, R + 16), lanes]
-        return remote(tsend, dst, sent.at[0], came.at[0], at_q(peer))
+        pl.semaphore_wait(barrier, 46)
+
+    mine = pl.ds(pl.multiple_of(m * R, R), R)
+
+    def tan_copy(to):
+        return remote(
+            tsend, tfull.at[xl, pl.ds(0, R + 16), mine], sent.at[0], came.at[0], to
+        )
 
     def own_copy(d, k):
         return remote(
-            dsend, dblk.at[c, z], sent.at[k], came.at[k], {"z": (z + d) % NZ}
+            dsend, dblk.at[c, z], sent.at[k], came.at[k], {"z": wrap(z + d, NZ)}
         )
 
     def pass_copy(block, d):
-        part = dblk.at[c, (z + block) % NZ]
-        return remote(part, part, sent.at[2], came.at[2], {"z": (z + d) % NZ})
+        part = dblk.at[c, wrap(z + block, NZ)]
+        return remote(part, part, sent.at[2], came.at[2], {"z": wrap(z + d, NZ)})
 
     def half_copy(side):
         return remote(dblk.at[side], dblk.at[side], sent.at[3], came.at[3], partner)
@@ -196,13 +205,16 @@
             jsend.at[cc * NZ + zz], jbuf.at[b], sent.at[4], came.at[4], {"z": zz, "c": cc}
         )
 
-    def start(n, me, copy):
-        with jax.named_scope(copy.__name__ + "_start"):
-            each(n - 1, lambda t: copy((me + t + 1) % n, me).start())
+    def start_jac(ds):
+        for d in ds:
+            for cc in range(2):
+                jac_copy(wrap(z + d, NZ), cc).start()
 
     def start_z(copy):
-        with jax.named_scope(copy.__name__ + "_start"):
-            each(NZ - 1, lambda t: copy((z + far_first(t)) % NZ, z).start())
+        for d in FAR_FIRST:
+            copy(wrap(z + d, NZ)).start()
+
+    xside = {"xl": 1 - xl}
 
     def recv(k, ref):
         with jax.named_scope(f"recv{k}"):
@@ -210,17 +222,12 @@
 
     def left(k, ref):
         remote(ref, ref, sent.at[k], came.at[k], partner).wait_send()
-
-    def start_jac(t):
-        zz = (z + far_first(t)) % NZ
-        for cc in range(2):
-            jac_copy(zz, cc).start()
 
     for d in (5, 11):
         own_copy(d, 1).start()
     for d in (1, 15, 2, 14):
         own_copy(d, 16).start()
-    each(5, start_jac)
+    start_jac(FAR_FIRST[0:5])
 
     own = ids_ref[z * 4 + c * 2 + xl]
     x_hot = (lax.broadcasted_iota(jnp.int32, (16, 512), 1) == own).astype(F32).astype(BF)
@@ -241,17 +248,17 @@
     top = lax.broadcasted_iota(jnp.int32, (16, R), 0) == 0
     tsend[0:R, :] = (hidden_slope * hidden_lin).astype(BF)
     tsend[R : R + 16, :] = jnp.where(top, jnp.broadcast_to(hidden_act, (16, R)), 0.0).astype(BF)
-    start(16, q, tan_copy)
-    mine = pl.ds(pl.multiple_of(m * R, R), R)
+    for d in PLANE:
+        tan_copy(plane(d)[1]).start()
     tfull[xl, 0 : R + 16, mine] = tsend[...]
 
     recv(1, dblk.at[0, pl.ds(0, 2)])
     for d in (2, 14, 1, 15):
         for block in (5, 11):
             pass_copy(block, d).start()
-    side = 1 - 2 * (z % 2)
-    pass_copy(NZ - 5 * side, NZ + 3 * side).start()
-    each(10, lambda t: start_jac(t + 5))
+    odd = z % 2
+    pass_copy(11 - 6 * odd, 3 + 10 * odd).start()
+    start_jac(FAR_FIRST[5:])
     jac_copy(z, 1 - c).start()
     recv(16, dblk.at[0, pl.ds(0, 4)])
     recv(2, dblk.at[0, pl.ds(0, 9)])
@@ -262,31 +269,32 @@
         dmat[rows, :] = dblk[side].astype(F32).reshape(R, WIDE).astype(BF)
 
     unpack(c)
-    recv(0, rbuf.at[pl.ds(0, 15)])
-    recv(4, jbuf.at[pl.ds(0, 31)])
+    recv(0, tbytes.at[pl.ds(0, 15)])
     recv(3, dblk.at[0])
     unpack(1 - c)
 
     lane = lax.broadcasted_iota(jnp.int32, (2 * R, R), 1)
     tgt = dmat[:, H:].astype(F32)
     dec = dmat[:, 0:H]
-    miss = []
     for i in range(2):
         want = jnp.sum(jnp.where(lane == z * 4 + c * 2 + i, tgt, 0.0), axis=1, keepdims=True)
         want = jnp.where(lane == 0, jnp.broadcast_to(want, (2 * R, R)), 0.0)
+        out = dot(dec, tfull[i], NT)
+        net[i, :, 0:R] = out[:, 0:R]
+        net[i, :, R:] = out[:, R:] - want
+    recv(4, jbuf.at[pl.ds(0, 31)])
+    miss = []
+    for i in range(2):
         stored = jbuf[:, i].astype(F32).reshape(2 * R, R)
-        net = dot(dec, tfull[i], NT)
-        miss_i = (net - jnp.concatenate([stored, want], axis=1)).astype(BF)
+        miss_i = jnp.concatenate([net[i, :, 0:R] - stored, net[i, :, R:]], axis=1).astype(BF)
         miss.append(miss_i)
-        pbuf[i] = dot(miss_i, dec, TN)[0 : R + 16].astype(BF)
-
-    def back_copy(peer, src):
-        lanes = pl.ds(pl.multiple_of((peer // 2) * R, R), R)
-        return remote(
-            pbuf.at[peer % 2, :, lanes], rbuf.at[src], sent.at[5], came.at[5], at_q(peer)
-        )
-
-    start(16, q, back_copy)
+        back_i = dot(miss_i, dec, TN)[0 : R + 8]
+        for k in range(8):
+            part = back_i[:, R * k : R * k + R]
+            pbuf[2 * k + i] = part.reshape(17, 8, R).astype(BF)
+    for d in PLANE:
+        peer, to = plane(d)
+        remote(pbuf.at[peer], rbuf.at[q], sent.at[5], came.at[5], to).start()
 
     gown[...] = dot(miss[0], tfull[0]) + dot(miss[1], tfull[1])
     theirs = gown[pl.ds(pl.multiple_of((1 - c) * R, R), R), :]
@@ -296,17 +304,15 @@
     recv(6, grecv)
     hsend[...] = (ours + grecv[...].astype(F32)).astype(BF)
 
-    def gz_copy(peer, src):
-        return remote(
-            hsend.at[peer], hrecv.at[src], sent.at[7], came.at[7], at_z(peer)
-        )
+    def gz_copy(peer):
+        return remote(hsend.at[peer], hrecv.at[z], sent.at[7], came.at[7], {"z": peer})
 
     start_z(gz_copy)
     hrecv[z] = hsend[z]
 
     recv(5, rbuf.at[pl.ds(0, 15)])
-    rbuf[q] = pbuf[xl, :, mine]
-    back = jnp.sum(rbuf[...].astype(F32), axis=0)
+    rbuf[q] = pbuf[q]
+    back = jnp.sum(rbuf[...].astype(F32), axis=0).reshape(R + 8, R)
     tan_back = back[0:R]
     act_back = back[R : R + 1]
     lin_round = (tan_back * hidden_slope).astype(BF)
@@ -327,51 +333,50 @@
     pre_wide = jnp.concatenate([pre_back] * 8, axis=1)
     tail = jnp.where(line == 0, jnp.broadcast_to(pre_lower, (8, H)), 0.0)
     tail = tail + jnp.where((line == 1) & place, jnp.broadcast_to(pre_wide, (8, H)), 0.0)
-    for k in range(4):
-        fsend[k, 0:4] = fw[32 * k : 32 * k + 32].reshape(4, 8, H).astype(BF)
-        fsend[k, 4] = tail.astype(BF)
-
-    def f_copy(peer, src):
-        lanes = pl.ds(pl.multiple_of((peer // 4) * R, R), R)
-        return remote(
-            fsend.at[peer % 4, :, :, lanes], frecv.at[src], sent.at[9], came.at[9], at_w(peer)
-        )
-
-    start(32, w, f_copy)
-    frecv[w] = fsend[e, :, :, mine]
-
-    qsend[...] = dot(ft[...], both, TN).astype(BF).reshape(4, 2 * R, R)
-
-    def q_copy(peer, src):
-        return remote(qsend.at[peer], qrecv.at[src], sent.at[8], came.at[8], at_e(peer))
-
-    start(4, e, q_copy)
-    qrecv[e] = qsend[e]
-
-    recv(9, frecv.at[pl.ds(0, 31)])
+    for cc in range(2):
+        for k in range(16):
+            r0 = 64 * cc + 32 * (k % 2)
+            l0 = R * (k // 2)
+            fsend[cc, k, 0:4] = fw[r0 : r0 + 32, l0 : l0 + R].reshape(4, 8, R).astype(BF)
+            fsend[cc, k, 4] = tail[:, l0 : l0 + R].astype(BF)
+    remote(fsend.at[1 - c], fpart, sent.at[9], came.at[9], partner).start()
+    qsend[...] = dot(ft[...], both, TN).astype(BF).reshape(2, 4 * R, R)
+    remote(qsend.at[1 - c], qpart, sent.at[8], came.at[8], partner).start()
+    recv(9, fpart)
+    fsum[...] = (fsend[c].astype(F32) + fpart[...].astype(F32)).astype(BF)
+    for d in PLANE:
+        peer, to = plane(d)
+        remote(fsum.at[peer], frecv.at[q], sent.at[17], came.at[17], to).start()
+    frecv[q] = fsum[q]
+    recv(8, qpart)
+    halves = qsend[c].astype(F32) + qpart[...].astype(F32)
+    qsum[...] = halves.astype(BF).reshape(2, 2 * R, R)
+    remote(qsum.at[1 - xl], qrecv, sent.at[18], came.at[18], xside).start()
+
+    recv(17, frecv.at[pl.ds(0, 15)])
     ysend[...] = jnp.sum(frecv[...].astype(F32), axis=0).astype(BF)
     for t in range(5):
 
         @pl.when(z != t)
         def _():
-            remote(ysend.at[t], yrecv.at[z], sent.at[11], came.at[11], at_z(t)).start()
+            remote(ysend.at[t], yrecv.at[z], sent.at[11], came.at[11], {"z": t}).start()
 
         @pl.when(z == t)
         def _():
             yrecv[z] = ysend[t]
 
-    recv(8, qrecv.at[pl.ds(0, 3)])
-    quarter = jnp.sum(qrecv[...].astype(F32), axis=0)
+    recv(18, qrecv)
+    quarter = qsum[xl].astype(F32) + qrecv[...].astype(F32)
     zsend[...] = quarter.reshape(NZ, 2, 8, R).astype(BF)
 
-    def zr_copy(peer, src):
-        return remote(zsend.at[peer], zrecv.at[src], sent.at[10], came.at[10], at_z(peer))
+    def zr_copy(peer):
+        return remote(zsend.at[peer], zrecv.at[z], sent.at[10], came.at[10], {"z": peer})
 
     start_z(zr_copy)
     zrecv[z] = zsend[z]
 
-    def y_copy(peer, src):
-        return remote(yall.at[src], yall.at[src], sent.at[13], came.at[13], at_z(peer))
+    def y_copy(peer):
+        return remote(yall.at[z], yall.at[z], sent.at[13], came.at[13], {"z": peer})
 
     @pl.when(z < 5)
     def _():
@@ -382,8 +387,8 @@
     recv(10, zrecv.at[pl.ds(0, 15)])
     zall[z] = jnp.sum(zrecv[...].astype(F32), axis=0).astype(BF)
 
-    def zg_copy(peer, src):
-        return remote(zall.at[src], zall.at[src], sent.at[12], came.at[12], at_z(peer))
+    def zg_copy(peer):
+        return remote(zall.at[z], zall.at[z], sent.at[12], came.at[12], {"z": peer})
 
     start_z(zg_copy)
 
@@ -405,27 +410,26 @@
     def _():
         recv(13, yall.at[pl.ds(0, 5)])
 
-    def fa_copy(peer, src):
-        return remote(yall.at[pl.ds(0, 5)], fall.at[src], sent.at[15], came.at[15], at_w(peer))
-
-    start(32, w, fa_copy)
-
-    recv(12, zall.at[pl.ds(0, 15)])
-
-    def h_copy(peer, src):
-        return remote(zall, hall.at[src], sent.at[14], came.at[14], at_e(peer))
-
-    start(4, e, h_copy)
-    hall[e] = zall[...]
-    fall[w] = yall[0:5]
+    for d in PLANE:
+        remote(
+            yall.at[pl.ds(0, 5)], fall.at[c, q], sent.at[15], came.at[15], plane(d)[1]
+        ).start()
+    fall[c, q] = yall[0:5]
     tile[...] = yall[4]
     outs[1].start()
-    recv(14, hall.at[pl.ds(0, 3)])
+    recv(12, zall.at[pl.ds(0, 15)])
+    remote(zall, hall.at[c, xl], sent.at[14], came.at[14], xside).start()
+    hall[c, xl] = zall[...]
+    recv(15, fall.at[0, pl.ds(0, 15)])
+    remote(fall.at[c], fall.at[c], sent.at[19], came.at[19], partner).start()
+    recv(14, zall)
+    remote(hall.at[c], hall.at[c], sent.at[20], came.at[20], partner).start()
+    recv(19, fall.at[0])
+    outs[3].start()
+    recv(20, hall.at[0])
     outs[2].start()
-    recv(15, fall.at[pl.ds(0, 31)])
-    outs[3].start()
-
-    left(0, rbuf.at[pl.ds(0, 15)])
+
+    left(0, tbytes.at[pl.ds(0, 15)])
     left(1, dblk.at[0, pl.ds(0, 2)])
     left(16, dblk.at[0, pl.ds(0, 4)])
     left(2, dblk.at[0, pl.ds(0, 9)])
@@ -434,8 +438,10 @@
     left(5, rbuf.at[pl.ds(0, 15)])
     left(6, grecv)
     left(7, hrecv.at[pl.ds(0, 15)])
-    left(8, qrecv.at[pl.ds(0, 3)])
-    left(9, frecv.at[pl.ds(0, 31)])
+    left(8, qpart)
+    left(9, fpart)
+    left(17, frecv.at[pl.ds(0, 15)])
+    left(18, qrecv)
     left(10, zrecv.at[pl.ds(0, 15)])
 
     @pl.when(z < 5)
@@ -448,8 +454,10 @@
         left(11, yall.at[pl.ds(0, 5)])
 
     left(12, zrecv.at[pl.ds(0, 15)])
-    left(14, hall.at[pl.ds(0, 3)])
-    left(15, fall.at[pl.ds(0, 31)])
+    left(14, zall)
+    left(15, fall.at[0, pl.ds(0, 15)])
+    left(19, fall.at[0])
+    left(20, hall.at[0])
     for out in outs:
         out.wait()
 
@@ -496,7 +504,7 @@
     ins[1].wait()
     for mm in range(8):
         for ee in range(4):
-            piece = fall[4 * mm + ee].astype(F32)
+            piece = fall[ee // 2, 2 * mm + ee % 2].astype(F32)
             fw[32 * ee : 32 * ee + 32, R * mm : R * mm + R] = piece[0:4].reshape(32, R)
             if ee == 0:
                 fb[mm : mm + 1, :] = piece[4, 0:1]
@@ -526,8 +534,8 @@
     smem = pl.BlockSpec(memory_space=pltpu.SMEM)
     hbm = pl.BlockSpec(memory_space=pltpu.HBM)
     dma = pltpu.SemaphoreType.DMA
-    hall = jax.ShapeDtypeStruct((4, NZ, 2, 8, R), BF)
-    fall = jax.ShapeDtypeStruct((32, 5, 8, R), BF)
+    hall = jax.ShapeDtypeStruct((2, 2, NZ, 2, 8, R), BF)
+    fall = jax.ShapeDtypeStruct((2, 16, 5, 8, R), BF)
     tile = jax.ShapeDtypeStruct((8, R), BF)
     dg = jax.ShapeDtypeStruct((8, H), F32)
     raw = (hall, fall, tile, dg)
@@ -553,29 +561,35 @@
             pltpu.VMEM((2 * R, WIDE), BF),
             pltpu.VMEM((32, 2, 8, R), BF),
             pltpu.VMEM((32, 2, 8, R), BF),
-            pltpu.VMEM((2, R + 16, H), BF),
+            pltpu.VMEM((2, 2 * R, 2 * R), F32),
             pltpu.VMEM((16, R + 16, R), BF),
+            pltpu.VMEM((16, 17, 8, R), BF),
+            pltpu.VMEM((16, 17, 8, R), BF),
             pltpu.VMEM((NZ, 8, H), BF),
             pltpu.VMEM((NZ, 8, H), BF),
             pltpu.VMEM((2 * R, H), F32),
             pltpu.VMEM((NZ, 8, H), BF),
             pltpu.VMEM((NZ, 8, H), BF),
-            pltpu.VMEM((4, 2 * R, R), BF),
-            pltpu.VMEM((4, 2 * R, R), BF),
-            pltpu.VMEM((4, 5, 8, H), BF),
-            pltpu.VMEM((32, 5, 8, R), BF),
+            pltpu.VMEM((2, 4 * R, R), BF),
+            pltpu.VMEM((4 * R, R), BF),
+            pltpu.VMEM((2, 2 * R, R), BF),
+            pltpu.VMEM((2 * R, R), BF),
+            pltpu.VMEM((2, 16, 5, 8, R), BF),
+            pltpu.VMEM((16, 5, 8, R), BF),
+            pltpu.VMEM((16, 5, 8, R), BF),
+            pltpu.VMEM((16, 5, 8, R), BF),
             pltpu.VMEM((NZ, 2, 8, R), BF),
             pltpu.VMEM((NZ, 2, 8, R), BF),
             pltpu.VMEM((NZ, 2, 8, R), BF),
             pltpu.VMEM((5, 8, R), BF),
             pltpu.VMEM((NZ, 8, R), BF),
             pltpu.VMEM((NZ, 8, R), BF),
-            pltpu.VMEM((4, NZ, 2, 8, R), BF),
-            pltpu.VMEM((32, 5, 8, R), BF),
+            pltpu.VMEM((2, 2, NZ, 2, 8, R), BF),
+            pltpu.VMEM((2, 16, 5, 8, R), BF),
             pltpu.VMEM((8, R), BF),
             pltpu.VMEM((8, H), F32),
-            dma((17,)),
-            dma((17,)),
+            dma((21,)),
+            dma((21,)),
             dma((8,)),
             dma((4,)),
         ],

time: 74.6 us -> 72.9 us (0.977)
  Pallas kernels: 73.8 us -> 72.1 us
    pallas_call x1, Pallas kernels: 71.8 us -> 70.1 us  [on_device(): pl.pallas_call(kernel, out_shape=raw, in_specs=[smem, vmem] + [hbm] * 8,...]
where the time goes in v4:
time: 72.9 us; the launch traced here: 72.8 us
  Pallas kernels  72.1 us (99%)
    pallas_call x1, Pallas kernels, on_device(): pl.pallas_call(kernel, out_shape=raw, in_specs=[smem, vmem] + [hbm] * 8,...  70.1 us
    pallas_call x1, Pallas kernels, on_device(): pl.pallas_call(unfold, out_shape=final, in_specs=[hbm] * 4, out_specs=(hb...  2.04 us

profile of v4, /device:TPU:1, one launch (start us, length us, event | category | flops | bytes accessed | tf_op | source)
XLA Modules:
  0.0 72.8 jit_solution(3649640731258777727)
XLA Ops:
  0.6 70.1 %shard_map.128 = (bf16[2,2,16,2,8,128]{5,4,3,2,1,0:T(8,128)(2,1)}, bf16[2,16,5,8,128]{4,3,2,1,0:T(8,128)(2,1)}, bf16[8,128]{1,0:T(8,128)(2,1)}, f32[8,1024]{1,0:T(8,128)}) custom-call(s32[64]{0:T(128)} %ids_ref.1, s32[1,64]{1,0:T(1,128)} %bitcast.8, bf16[512,128]{1,0:T(8,128)(2,1)} %xs_hbm.1, bf16[512,8,128]{2,1,0:T(8,128)(2,1)} %jac_hbm.1, ...), custom_call_target="tpu_custom_call" | custom-call | tf_op jit(solution)/shard_map/pallas_call | solution.py:542
  70.7 2.0 %shard_map.129 = (f32[128,1024]{1,0:T(8,128)}, f32[8,128]{1,0:T(8,128)}, f32[1024,128]{1,0:T(8,128)}, f32[1,128]{1,0:T(1,128)}, f32[8,1024]{1,0:T(8,128)}) custom-call(bf16[2,2,16,2,8,128]{5,4,3,2,1,0:T(8,128)(2,1)} %get-tuple-element.14.hall_hbm, bf16[2,16,5,8,128]{4,3,2,1,0:T(8,128)(2,1)} %get-tuple-element.15.fall_hbm, ...), custom_call_target="tpu_custom_call" | custom-call | tf_op jit(solution)/shard_map/pallas_call | solution.py:618

commit v5 on v4

--- a/solution.py
+++ b/solution.py
@@ -137,9 +137,9 @@
     barrier = pltpu.get_barrier_semaphore()
 
     homes = (
-        (jac_hbm, jac_ref),
         (tgt_hbm, tgt_ref),
         (dec_hbm, dec_ref),
+        (jac_hbm, jac_ref),
         (xs_hbm, xs_ref),
         (w1_hbm, w1_ref),
         (hw_hbm, hw_ref),
@@ -149,6 +149,7 @@
     loads = [pltpu.make_async_copy(a, v, taken.at[k]) for k, (a, v) in enumerate(homes)]
     for load in loads:
         load.start()
+
     def greet(to):
         pl.semaphore_signal(barrier, inc=1, device_id=to, device_id_type=MESH)
 
@@ -159,24 +160,12 @@
         greet(plane(d)[1])
     greet(partner)
 
-    tfull[:, R + 16 :, :] = jnp.zeros((2, 2 * R - R - 16, H), BF)
     hot = (lax.broadcasted_iota(jnp.int32, (512, 64), 0) == idv_ref[...]).astype(F32).astype(BF)
-    for load in loads[0:3]:
+    for load in loads[0:2]:
         load.wait()
-
-    def pick(zz):
-        for cc in range(2):
-            for i in range(2):
-                jsend[cc * NZ + zz, i] = jac_ref[ids_ref[zz * 4 + cc * 2 + i]]
-
-    each(NZ, pick)
     dsend[:, 0:H] = dec_ref[...]
     dsend[:, H : H + 64] = dot(tgt_ref[...], hot).astype(BF)
     dsend[:, H + 64 :] = jnp.zeros((8, R - 64), BF)
-    dblk[c, z] = dsend[...]
-    jbuf[b] = jsend[b]
-    for load in loads[3:]:
-        load.wait()
 
     with jax.named_scope("barrier"):
         pl.semaphore_wait(barrier, 46)
@@ -200,15 +189,20 @@
     def half_copy(side):
         return remote(dblk.at[side], dblk.at[side], sent.at[3], came.at[3], partner)
 
-    def jac_copy(zz, cc):
+    def jac_copy(zz, cc, i):
         return remote(
-            jsend.at[cc * NZ + zz], jbuf.at[b], sent.at[4], came.at[4], {"z": zz, "c": cc}
+            jsend.at[i, cc * NZ + zz],
+            jbuf.at[i, b],
+            sent.at[4 if i == 0 else 21],
+            came.at[4 if i == 0 else 21],
+            {"z": zz, "c": cc},
         )
 
-    def start_jac(ds):
-        for d in ds:
+    def start_jac(i):
+        for d in FAR_FIRST:
             for cc in range(2):
-                jac_copy(wrap(z + d, NZ), cc).start()
+                jac_copy(wrap(z + d, NZ), cc, i).start()
+        jac_copy(z, 1 - c, i).start()
 
     def start_z(copy):
         for d in FAR_FIRST:
@@ -227,7 +221,21 @@
         own_copy(d, 1).start()
     for d in (1, 15, 2, 14):
         own_copy(d, 16).start()
-    start_jac(FAR_FIRST[0:5])
+    dblk[c, z] = dsend[...]
+    loads[2].wait()
+
+    def pick(zz):
+        for cc in range(2):
+            for i in range(2):
+                jsend[i, cc * NZ + zz] = jac_ref[ids_ref[zz * 4 + cc * 2 + i]]
+
+    with jax.named_scope("pick"):
+        each(NZ, pick)
+    start_jac(0)
+    for i in range(2):
+        jbuf[i, b] = jsend[i, b]
+    for load in loads[3:]:
+        load.wait()
 
     own = ids_ref[z * 4 + c * 2 + xl]
     x_hot = (lax.broadcasted_iota(jnp.int32, (16, 512), 1) == own).astype(F32).astype(BF)
@@ -250,6 +258,7 @@
     tsend[R : R + 16, :] = jnp.where(top, jnp.broadcast_to(hidden_act, (16, R)), 0.0).astype(BF)
     for d in PLANE:
         tan_copy(plane(d)[1]).start()
+    tfull[:, R + 16 :, :] = jnp.zeros((2, 2 * R - R - 16, H), BF)
     tfull[xl, 0 : R + 16, mine] = tsend[...]
 
     recv(1, dblk.at[0, pl.ds(0, 2)])
@@ -258,8 +267,7 @@
             pass_copy(block, d).start()
     odd = z % 2
     pass_copy(11 - 6 * odd, 3 + 10 * odd).start()
-    start_jac(FAR_FIRST[5:])
-    jac_copy(z, 1 - c).start()
+    start_jac(1)
     recv(16, dblk.at[0, pl.ds(0, 4)])
     recv(2, dblk.at[0, pl.ds(0, 9)])
     half_copy(c).start()
@@ -282,19 +290,30 @@
         out = dot(dec, tfull[i], NT)
         net[i, :, 0:R] = out[:, 0:R]
         net[i, :, R:] = out[:, R:] - want
-    recv(4, jbuf.at[pl.ds(0, 31)])
     miss = []
     for i in range(2):
-        stored = jbuf[:, i].astype(F32).reshape(2 * R, R)
+        recv(4 if i == 0 else 21, jbuf.at[0, pl.ds(0, 31)])
+        stored = jbuf[i].astype(F32).reshape(2 * R, R)
         miss_i = jnp.concatenate([net[i, :, 0:R] - stored, net[i, :, R:]], axis=1).astype(BF)
         miss.append(miss_i)
         back_i = dot(miss_i, dec, TN)[0 : R + 8]
         for k in range(8):
             part = back_i[:, R * k : R * k + R]
-            pbuf[2 * k + i] = part.reshape(17, 8, R).astype(BF)
-    for d in PLANE:
-        peer, to = plane(d)
-        remote(pbuf.at[peer], rbuf.at[q], sent.at[5], came.at[5], to).start()
+            pbuf[i, k] = part.reshape(17, 8, R).astype(BF)
+        for dy in (2, 1, 3, 0):
+            for hh in range(2):
+                yy = wrap(y + dy, 4)
+                to = {"y": yy, "xh": hh, "xl": i}
+
+                def send():
+                    remote(
+                        pbuf.at[i, yy * 2 + hh], rbuf.at[q], sent.at[5], came.at[5], to
+                    ).start()
+
+                if dy:
+                    send()
+                else:
+                    pl.when((hh != xh) | (xl != i))(send)
 
     gown[...] = dot(miss[0], tfull[0]) + dot(miss[1], tfull[1])
     theirs = gown[pl.ds(pl.multiple_of((1 - c) * R, R), R), :]
@@ -311,7 +330,7 @@
     hrecv[z] = hsend[z]
 
     recv(5, rbuf.at[pl.ds(0, 15)])
-    rbuf[q] = pbuf[q]
+    rbuf[q] = pbuf[xl, m]
     back = jnp.sum(rbuf[...].astype(F32), axis=0).reshape(R + 8, R)
     tan_back = back[0:R]
     act_back = back[R : R + 1]
@@ -434,7 +453,8 @@
     left(16, dblk.at[0, pl.ds(0, 4)])
     left(2, dblk.at[0, pl.ds(0, 9)])
     left(3, dblk.at[0])
-    left(4, jbuf.at[pl.ds(0, 31)])
+    left(4, jbuf.at[0, pl.ds(0, 31)])
+    left(21, jbuf.at[0, pl.ds(0, 31)])
     left(5, rbuf.at[pl.ds(0, 15)])
     left(6, grecv)
     left(7, hrecv.at[pl.ds(0, 15)])
@@ -559,11 +579,11 @@
             pltpu.VMEM((8, WIDE), BF),
             pltpu.VMEM((2, NZ, 8, WIDE), BF),
             pltpu.VMEM((2 * R, WIDE), BF),
-            pltpu.VMEM((32, 2, 8, R), BF),
-            pltpu.VMEM((32, 2, 8, R), BF),
+            pltpu.VMEM((2, 32, 8, R), BF),
+            pltpu.VMEM((2, 32, 8, R), BF),
             pltpu.VMEM((2, 2 * R, 2 * R), F32),
             pltpu.VMEM((16, R + 16, R), BF),
-            pltpu.VMEM((16, 17, 8, R), BF),
+            pltpu.VMEM((2, 8, 17, 8, R), BF),
             pltpu.VMEM((16, 17, 8, R), BF),
             pltpu.VMEM((NZ, 8, H), BF),
             pltpu.VMEM((NZ, 8, H), BF),
@@ -588,8 +608,8 @@
             pltpu.VMEM((2, 16, 5, 8, R), BF),
             pltpu.VMEM((8, R), BF),
             pltpu.VMEM((8, H), F32),
-            dma((21,)),
-            dma((21,)),
+            dma((22,)),
+            dma((22,)),
             dma((8,)),
             dma((4,)),
         ],

time: 72.9 us -> 74.2 us (1.018)
  Pallas kernels: 72.1 us -> 73.4 us
    pallas_call x1, Pallas kernels: 70.1 us -> 71.3 us  [on_device(): pl.pallas_call(kernel, out_shape=raw, in_specs=[smem, vmem] + [hbm] * 8,...]
where the time goes in v5:
time: 74.2 us; the launch traced here: 74 us
  Pallas kernels  73.4 us (99%)
    pallas_call x1, Pallas kernels, on_device(): pl.pallas_call(kernel, out_shape=raw, in_specs=[smem, vmem] + [hbm] * 8,...  71.3 us
    pallas_call x1, Pallas kernels, on_device(): pl.pallas_call(unfold, out_shape=final, in_specs=[hbm] * 4, out_specs=(hb...  2.04 us

profile of v5, /device:TPU:1, one launch (start us, length us, event | category | flops | bytes accessed | tf_op | source)
XLA Modules:
  0.0 74.0 jit_solution(13899218861457321899)
XLA Ops:
  0.6 71.3 %shard_map.128 = (bf16[2,2,16,2,8,128]{5,4,3,2,1,0:T(8,128)(2,1)}, bf16[2,16,5,8,128]{4,3,2,1,0:T(8,128)(2,1)}, bf16[8,128]{1,0:T(8,128)(2,1)}, f32[8,1024]{1,0:T(8,128)}) custom-call(s32[64]{0:T(128)} %ids_ref.1, s32[1,64]{1,0:T(1,128)} %bitcast.8, bf16[512,128]{1,0:T(8,128)(2,1)} %xs_hbm.1, bf16[512,8,128]{2,1,0:T(8,128)(2,1)} %jac_hbm.1, ...), custom_call_target="tpu_custom_call" | custom-call | tf_op jit(solution)/shard_map/pallas_call | solution.py:562
  72.0 2.0 %shard_map.129 = (f32[128,1024]{1,0:T(8,128)}, f32[8,128]{1,0:T(8,128)}, f32[1024,128]{1,0:T(8,128)}, f32[1,128]{1,0:T(1,128)}, f32[8,1024]{1,0:T(8,128)}) custom-call(bf16[2,2,16,2,8,128]{5,4,3,2,1,0:T(8,128)(2,1)} %get-tuple-element.14.hall_hbm, bf16[2,16,5,8,128]{4,3,2,1,0:T(8,128)(2,1)} %get-tuple-element.15.fall_hbm, ...), custom_call_target="tpu_custom_call" | custom-call | tf_op jit(solution)/shard_map/pallas_call | solution.py:638

commit v6 on v5

--- a/solution.py
+++ b/solution.py
@@ -189,20 +189,15 @@
     def half_copy(side):
         return remote(dblk.at[side], dblk.at[side], sent.at[3], came.at[3], partner)
 
-    def jac_copy(zz, cc, i):
+    def jac_copy(zz, cc):
         return remote(
-            jsend.at[i, cc * NZ + zz],
-            jbuf.at[i, b],
-            sent.at[4 if i == 0 else 21],
-            came.at[4 if i == 0 else 21],
-            {"z": zz, "c": cc},
+            jsend.at[cc * NZ + zz], jbuf.at[b], sent.at[4], came.at[4], {"z": zz, "c": cc}
         )
 
-    def start_jac(i):
-        for d in FAR_FIRST:
+    def start_jac(ds):
+        for d in ds:
             for cc in range(2):
-                jac_copy(wrap(z + d, NZ), cc, i).start()
-        jac_copy(z, 1 - c, i).start()
+                jac_copy(wrap(z + d, NZ), cc).start()
 
     def start_z(copy):
         for d in FAR_FIRST:
@@ -227,13 +222,11 @@
     def pick(zz):
         for cc in range(2):
             for i in range(2):
-                jsend[i, cc * NZ + zz] = jac_ref[ids_ref[zz * 4 + cc * 2 + i]]
-
-    with jax.named_scope("pick"):
-        each(NZ, pick)
-    start_jac(0)
-    for i in range(2):
-        jbuf[i, b] = jsend[i, b]
+                jsend[cc * NZ + zz, i] = jac_ref[ids_ref[zz * 4 + cc * 2 + i]]
+
+    each(NZ, pick)
+    start_jac(FAR_FIRST[0:5])
+    jbuf[b] = jsend[b]
     for load in loads[3:]:
         load.wait()
 
@@ -267,7 +260,8 @@
             pass_copy(block, d).start()
     odd = z % 2
     pass_copy(11 - 6 * odd, 3 + 10 * odd).start()
-    start_jac(1)
+    start_jac(FAR_FIRST[5:])
+    jac_copy(z, 1 - c).start()
     recv(16, dblk.at[0, pl.ds(0, 4)])
     recv(2, dblk.at[0, pl.ds(0, 9)])
     half_copy(c).start()
@@ -290,10 +284,10 @@
         out = dot(dec, tfull[i], NT)
         net[i, :, 0:R] = out[:, 0:R]
         net[i, :, R:] = out[:, R:] - want
+    recv(4, jbuf.at[pl.ds(0, 31)])
     miss = []
     for i in range(2):
-        recv(4 if i == 0 else 21, jbuf.at[0, pl.ds(0, 31)])
-        stored = jbuf[i].astype(F32).reshape(2 * R, R)
+        stored = jbuf[:, i].astype(F32).reshape(2 * R, R)
         miss_i = jnp.concatenate([net[i, :, 0:R] - stored, net[i, :, R:]], axis=1).astype(BF)
         miss.append(miss_i)
         back_i = dot(miss_i, dec, TN)[0 : R + 8]
@@ -340,6 +334,9 @@
     )
     pre_round = jnp.where(top, jnp.broadcast_to(pre_back, (16, R)), 0.0).astype(BF)
     both = jnp.concatenate([lin_round, pre_round], axis=0)
+    qsend[...] = dot(ft[...], both, TN).astype(BF).reshape(2, 4 * R, R)
+    remote(qsend.at[1 - c], qpart, sent.at[8], came.at[8], partner).start()
+
     low = dot(both, hw_ref[...], NT)
     tan_lower = low[0:R]
     pre_lower = low[R : R + 1] * first_slope - 2.0 * first_act * first_slope * jnp.sum(
@@ -359,31 +356,16 @@
             fsend[cc, k, 0:4] = fw[r0 : r0 + 32, l0 : l0 + R].reshape(4, 8, R).astype(BF)
             fsend[cc, k, 4] = tail[:, l0 : l0 + R].astype(BF)
     remote(fsend.at[1 - c], fpart, sent.at[9], came.at[9], partner).start()
-    qsend[...] = dot(ft[...], both, TN).astype(BF).reshape(2, 4 * R, R)
-    remote(qsend.at[1 - c], qpart, sent.at[8], came.at[8], partner).start()
+    recv(8, qpart)
+    halves = qsend[c].astype(F32) + qpart[...].astype(F32)
+    qsum[...] = halves.astype(BF).reshape(2, 2 * R, R)
+    remote(qsum.at[1 - xl], qrecv, sent.at[18], came.at[18], xside).start()
     recv(9, fpart)
     fsum[...] = (fsend[c].astype(F32) + fpart[...].astype(F32)).astype(BF)
     for d in PLANE:
         peer, to = plane(d)
         remote(fsum.at[peer], frecv.at[q], sent.at[17], came.at[17], to).start()
     frecv[q] = fsum[q]
-    recv(8, qpart)
-    halves = qsend[c].astype(F32) + qpart[...].astype(F32)
-    qsum[...] = halves.astype(BF).reshape(2, 2 * R, R)
-    remote(qsum.at[1 - xl], qrecv, sent.at[18], came.at[18], xside).start()
-
-    recv(17, frecv.at[pl.ds(0, 15)])
-    ysend[...] = jnp.sum(frecv[...].astype(F32), axis=0).astype(BF)
-    for t in range(5):
-
-        @pl.when(z != t)
-        def _():
-            remote(ysend.at[t], yrecv.at[z], sent.at[11], came.at[11], {"z": t}).start()
-
-        @pl.when(z == t)
-        def _():
-            yrecv[z] = ysend[t]
-
     recv(18, qrecv)
     quarter = qsum[xl].astype(F32) + qrecv[...].astype(F32)
     zsend[...] = quarter.reshape(NZ, 2, 8, R).astype(BF)
@@ -394,14 +376,22 @@
     start_z(zr_copy)
     zrecv[z] = zsend[z]
 
-    def y_copy(peer):
-        return remote(yall.at[z], yall.at[z], sent.at[13], came.at[13], {"z": peer})
-
-    @pl.when(z < 5)
-    def _():
-        recv(11, yrecv.at[pl.ds(0, 15)])
-        yall[z] = jnp.sum(yrecv[...].astype(F32), axis=0).astype(BF)
-        start_z(y_copy)
+    recv(17, frecv.at[pl.ds(0, 15)])
+    ysend[...] = jnp.sum(frecv[...].astype(F32), axis=0).astype(BF)
+
+    def y_copy(d, k):
+        to = {"z": wrap(z + d, NZ)}
+        return remote(ysend, yrecv.at[z], sent.at[k], came.at[k], to)
+
+    def y_pass(block, d):
+        part = yrecv.at[wrap(z + block, NZ)]
+        return remote(part, part, sent.at[21], came.at[21], {"z": wrap(z + d, NZ)})
+
+    for d in (5, 11):
+        y_copy(d, 11).start()
+    for d in (1, 15, 2, 14):
+        y_copy(d, 13).start()
+    yrecv[z] = ysend[...]
 
     recv(10, zrecv.at[pl.ds(0, 15)])
     zall[z] = jnp.sum(zrecv[...].astype(F32), axis=0).astype(BF)
@@ -410,6 +400,12 @@
         return remote(zall.at[z], zall.at[z], sent.at[12], came.at[12], {"z": peer})
 
     start_z(zg_copy)
+
+    recv(11, yrecv.at[pl.ds(0, 2)])
+    for d in (2, 14, 1, 15):
+        for block in (5, 11):
+            y_pass(block, d).start()
+    y_pass(11 - 6 * odd, 3 + 10 * odd).start()
 
     recv(7, hrecv.at[pl.ds(0, 15)])
     dg_ref[...] = jnp.sum(hrecv[...].astype(F32), axis=0)
@@ -421,19 +417,12 @@
     )
     outs[0].start()
 
-    @pl.when(z < 5)
-    def _():
-        recv(13, yall.at[pl.ds(0, 4)])
-
-    @pl.when(z >= 5)
-    def _():
-        recv(13, yall.at[pl.ds(0, 5)])
-
+    recv(13, yrecv.at[pl.ds(0, 4)])
+    recv(21, yrecv.at[pl.ds(0, 9)])
+    yall[...] = jnp.sum(yrecv[...].astype(F32), axis=0).astype(BF)
     for d in PLANE:
-        remote(
-            yall.at[pl.ds(0, 5)], fall.at[c, q], sent.at[15], came.at[15], plane(d)[1]
-        ).start()
-    fall[c, q] = yall[0:5]
+        remote(yall, fall.at[c, q], sent.at[15], came.at[15], plane(d)[1]).start()
+    fall[c, q] = yall[...]
     tile[...] = yall[4]
     outs[1].start()
     recv(12, zall.at[pl.ds(0, 15)])
@@ -453,8 +442,7 @@
     left(16, dblk.at[0, pl.ds(0, 4)])
     left(2, dblk.at[0, pl.ds(0, 9)])
     left(3, dblk.at[0])
-    left(4, jbuf.at[0, pl.ds(0, 31)])
-    left(21, jbuf.at[0, pl.ds(0, 31)])
+    left(4, jbuf.at[pl.ds(0, 31)])
     left(5, rbuf.at[pl.ds(0, 15)])
     left(6, grecv)
     left(7, hrecv.at[pl.ds(0, 15)])
@@ -464,15 +452,9 @@
     left(18, qrecv)
     left(10, zrecv.at[pl.ds(0, 15)])
 
-    @pl.when(z < 5)
-    def _():
-        left(11, yall.at[pl.ds(0, 4)])
-        left(13, yrecv.at[pl.ds(0, 15)])
-
-    @pl.when(z >= 5)
-    def _():
-        left(11, yall.at[pl.ds(0, 5)])
-
+    left(11, yrecv.at[pl.ds(0, 2)])
+    left(13, yrecv.at[pl.ds(0, 4)])
+    left(21, yrecv.at[pl.ds(0, 9)])
     left(12, zrecv.at[pl.ds(0, 15)])
     left(14, zall)
     left(15, fall.at[0, pl.ds(0, 15)])
@@ -579,8 +561,8 @@
             pltpu.VMEM((8, WIDE), BF),
             pltpu.VMEM((2, NZ, 8, WIDE), BF),
             pltpu.VMEM((2 * R, WIDE), BF),
-            pltpu.VMEM((2, 32, 8, R), BF),
-            pltpu.VMEM((2, 32, 8, R), BF),
+            pltpu.VMEM((32, 2, 8, R), BF),
+            pltpu.VMEM((32, 2, 8, R), BF),
             pltpu.VMEM((2, 2 * R, 2 * R), F32),
             pltpu.VMEM((16, R + 16, R), BF),
             pltpu.VMEM((2, 8, 17, 8, R), BF),
@@ -602,8 +584,8 @@
             pltpu.VMEM((NZ, 2, 8, R), BF),
             pltpu.VMEM((NZ, 2, 8, R), BF),
             pltpu.VMEM((5, 8, R), BF),
-            pltpu.VMEM((NZ, 8, R), BF),
-            pltpu.VMEM((NZ, 8, R), BF),
+            pltpu.VMEM((NZ, 5, 8, R), BF),
+            pltpu.VMEM((5, 8, R), BF),
             pltpu.VMEM((2, 2, NZ, 2, 8, R), BF),
             pltpu.VMEM((2, 16, 5, 8, R), BF),
             pltpu.VMEM((8, R), BF),

time: 74.2 us -> 72.9 us (0.982)
  Pallas kernels: 73.4 us -> 72.1 us
    pallas_call x1, Pallas kernels: 71.3 us -> 70 us  [on_device(): pl.pallas_call(kernel, out_shape=raw, in_specs=[smem, vmem] + [hbm] * 8,...]
where the time goes in v6:
time: 72.9 us; the launch traced here: 72.7 us
  Pallas kernels  72.1 us (99%)
    pallas_call x1, Pallas kernels, on_device(): pl.pallas_call(kernel, out_shape=raw, in_specs=[smem, vmem] + [hbm] * 8,...  70 us
    pallas_call x1, Pallas kernels, on_device(): pl.pallas_call(unfold, out_shape=final, in_specs=[hbm] * 4, out_specs=(hb...  2.04 us

profile of v6, /device:TPU:1, one launch (start us, length us, event | category | flops | bytes accessed | tf_op | source)
XLA Modules:
  0.0 72.7 jit_solution(4050216159561187211)
XLA Ops:
  0.6 70.0 %shard_map.128 = (bf16[2,2,16,2,8,128]{5,4,3,2,1,0:T(8,128)(2,1)}, bf16[2,16,5,8,128]{4,3,2,1,0:T(8,128)(2,1)}, bf16[8,128]{1,0:T(8,128)(2,1)}, f32[8,1024]{1,0:T(8,128)}) custom-call(s32[64]{0:T(128)} %ids_ref.1, s32[1,64]{1,0:T(1,128)} %bitcast.8, bf16[512,128]{1,0:T(8,128)(2,1)} %xs_hbm.1, bf16[512,8,128]{2,1,0:T(8,128)(2,1)} %jac_hbm.1, ...), custom_call_target="tpu_custom_call" | custom-call | tf_op jit(solution)/shard_map/pallas_call | solution.py:544
  70.7 2.0 %shard_map.129 = (f32[128,1024]{1,0:T(8,128)}, f32[8,128]{1,0:T(8,128)}, f32[1024,128]{1,0:T(8,128)}, f32[1,128]{1,0:T(1,128)}, f32[8,1024]{1,0:T(8,128)}) custom-call(bf16[2,2,16,2,8,128]{5,4,3,2,1,0:T(8,128)(2,1)} %get-tuple-element.14.hall_hbm, bf16[2,16,5,8,128]{4,3,2,1,0:T(8,128)(2,1)} %get-tuple-element.15.fall_hbm, ...), custom_call_target="tpu_custom_call" | custom-call | tf_op jit(solution)/shard_map/pallas_call | solution.py:620

commit v7 on v6

--- a/solution.py
+++ b/solution.py
@@ -214,7 +214,7 @@
 
     for d in (5, 11):
         own_copy(d, 1).start()
-    for d in (1, 15, 2, 14):
+    for d in (1, 15):
         own_copy(d, 16).start()
     dblk[c, z] = dsend[...]
     loads[2].wait()
@@ -254,6 +254,9 @@
     tfull[:, R + 16 :, :] = jnp.zeros((2, 2 * R - R - 16, H), BF)
     tfull[xl, 0 : R + 16, mine] = tsend[...]
 
+    recv(16, dblk.at[0, pl.ds(0, 2)])
+    pass_copy(15, 1).start()
+    pass_copy(1, 15).start()
     recv(1, dblk.at[0, pl.ds(0, 2)])
     for d in (2, 14, 1, 15):
         for block in (5, 11):
@@ -262,8 +265,7 @@
     pass_copy(11 - 6 * odd, 3 + 10 * odd).start()
     start_jac(FAR_FIRST[5:])
     jac_copy(z, 1 - c).start()
-    recv(16, dblk.at[0, pl.ds(0, 4)])
-    recv(2, dblk.at[0, pl.ds(0, 9)])
+    recv(2, dblk.at[0, pl.ds(0, 11)])
     half_copy(c).start()
 
     def unpack(side):
@@ -393,27 +395,27 @@
         y_copy(d, 13).start()
     yrecv[z] = ysend[...]
 
-    recv(10, zrecv.at[pl.ds(0, 15)])
-    zall[z] = jnp.sum(zrecv[...].astype(F32), axis=0).astype(BF)
-
-    def zg_copy(peer):
-        return remote(zall.at[z], zall.at[z], sent.at[12], came.at[12], {"z": peer})
-
-    start_z(zg_copy)
-
     recv(11, yrecv.at[pl.ds(0, 2)])
     for d in (2, 14, 1, 15):
         for block in (5, 11):
             y_pass(block, d).start()
     y_pass(11 - 6 * odd, 3 + 10 * odd).start()
 
+    recv(10, zrecv.at[pl.ds(0, 15)])
+    zall[z] = jnp.sum(zrecv[...].astype(F32), axis=0).astype(BF)
+
+    def zg_copy(peer):
+        return remote(zall.at[z], zall.at[z], sent.at[12], came.at[12], {"z": peer})
+
+    start_z(zg_copy)
+
     recv(7, hrecv.at[pl.ds(0, 15)])
     dg_ref[...] = jnp.sum(hrecv[...].astype(F32), axis=0)
     outs = (
         pltpu.make_async_copy(dg_ref, dg_hbm, put.at[0]),
         pltpu.make_async_copy(tile, tile_hbm, put.at[1]),
-        pltpu.make_async_copy(hall, hall_hbm, put.at[2]),
-        pltpu.make_async_copy(fall, fall_hbm, put.at[3]),
+        pltpu.make_async_copy(hall, hall_hbm.at[c], put.at[2]),
+        pltpu.make_async_copy(fall, fall_hbm.at[c], put.at[3]),
     )
     outs[0].start()
 
@@ -421,26 +423,26 @@
     recv(21, yrecv.at[pl.ds(0, 9)])
     yall[...] = jnp.sum(yrecv[...].astype(F32), axis=0).astype(BF)
     for d in PLANE:
-        remote(yall, fall.at[c, q], sent.at[15], came.at[15], plane(d)[1]).start()
-    fall[c, q] = yall[...]
+        remote(yall, fall.at[q], sent.at[15], came.at[15], plane(d)[1]).start()
+    fall[q] = yall[...]
     tile[...] = yall[4]
     outs[1].start()
     recv(12, zall.at[pl.ds(0, 15)])
-    remote(zall, hall.at[c, xl], sent.at[14], came.at[14], xside).start()
-    hall[c, xl] = zall[...]
-    recv(15, fall.at[0, pl.ds(0, 15)])
-    remote(fall.at[c], fall.at[c], sent.at[19], came.at[19], partner).start()
+    remote(zall, hall.at[xl], sent.at[14], came.at[14], xside).start()
+    hall[xl] = zall[...]
+    recv(15, fall.at[pl.ds(0, 15)])
+    remote(fall, fall_hbm.at[c], sent.at[19], came.at[19], partner).start()
+    outs[3].start()
     recv(14, zall)
-    remote(hall.at[c], hall.at[c], sent.at[20], came.at[20], partner).start()
-    recv(19, fall.at[0])
-    outs[3].start()
-    recv(20, hall.at[0])
+    remote(hall, hall_hbm.at[c], sent.at[20], came.at[20], partner).start()
     outs[2].start()
+    recv(19, fall)
+    recv(20, hall)
 
     left(0, tbytes.at[pl.ds(0, 15)])
     left(1, dblk.at[0, pl.ds(0, 2)])
-    left(16, dblk.at[0, pl.ds(0, 4)])
-    left(2, dblk.at[0, pl.ds(0, 9)])
+    left(16, dblk.at[0, pl.ds(0, 2)])
+    left(2, dblk.at[0, pl.ds(0, 11)])
     left(3, dblk.at[0])
     left(4, jbuf.at[pl.ds(0, 31)])
     left(5, rbuf.at[pl.ds(0, 15)])
@@ -457,9 +459,9 @@
     left(21, yrecv.at[pl.ds(0, 9)])
     left(12, zrecv.at[pl.ds(0, 15)])
     left(14, zall)
-    left(15, fall.at[0, pl.ds(0, 15)])
-    left(19, fall.at[0])
-    left(20, hall.at[0])
+    left(15, fall.at[pl.ds(0, 15)])
+    left(19, fall)
+    left(20, hall)
     for out in outs:
         out.wait()
 
@@ -586,8 +588,8 @@
             pltpu.VMEM((5, 8, R), BF),
             pltpu.VMEM((NZ, 5, 8, R), BF),
             pltpu.VMEM((5, 8, R), BF),
-            pltpu.VMEM((2, 2, NZ, 2, 8, R), BF),
-            pltpu.VMEM((2, 16, 5, 8, R), BF),
+            pltpu.VMEM((2, NZ, 2, 8, R), BF),
+            pltpu.VMEM((16, 5, 8, R), BF),
             pltpu.VMEM((8, R), BF),
             pltpu.VMEM((8, H), F32),
             dma((22,)),

time: 72.9 us -> 73 us (level)
  no operation moved by 1% of the time
where the time goes in v7:
time: 73 us; the launch traced here: 72.8 us
  Pallas kernels  72.1 us (99%)
    pallas_call x1, Pallas kernels, on_device(): pl.pallas_call(kernel, out_shape=raw, in_specs=[smem, vmem] + [hbm] * 8,...  70.1 us
    pallas_call x1, Pallas kernels, on_device(): pl.pallas_call(unfold, out_shape=final, in_specs=[hbm] * 4, out_specs=(hb...  2.04 us

profile of v7, /device:TPU:1, one launch (start us, length us, event | category | flops | bytes accessed | tf_op | source)
XLA Modules:
  0.0 72.8 jit_solution(9961970302027286576)
XLA Ops:
  0.6 70.1 %shard_map.128 = (bf16[2,2,16,2,8,128]{5,4,3,2,1,0:T(8,128)(2,1)}, bf16[2,16,5,8,128]{4,3,2,1,0:T(8,128)(2,1)}, bf16[8,128]{1,0:T(8,128)(2,1)}, f32[8,1024]{1,0:T(8,128)}) custom-call(s32[64]{0:T(128)} %ids_ref.1, s32[1,64]{1,0:T(1,128)} %bitcast.8, bf16[512,128]{1,0:T(8,128)(2,1)} %xs_hbm.1, bf16[512,8,128]{2,1,0:T(8,128)(2,1)} %jac_hbm.1, ...), custom_call_target="tpu_custom_call" | custom-call | tf_op jit(solution)/shard_map/pallas_call | solution.py:546
  70.7 2.0 %shard_map.129 = (f32[128,1024]{1,0:T(8,128)}, f32[8,128]{1,0:T(8,128)}, f32[1024,128]{1,0:T(8,128)}, f32[1,128]{1,0:T(1,128)}, f32[8,1024]{1,0:T(8,128)}) custom-call(bf16[2,2,16,2,8,128]{5,4,3,2,1,0:T(8,128)(2,1)} %get-tuple-element.14.hall_hbm, bf16[2,16,5,8,128]{4,3,2,1,0:T(8,128)(2,1)} %get-tuple-element.15.fall_hbm, ...), custom_call_target="tpu_custom_call" | custom-call | tf_op jit(solution)/shard_map/pallas_call | solution.py:622

commit v8 on v6

--- a/solution.py
+++ b/solution.py
@@ -45,6 +45,7 @@
 
 
 FAR_FIRST = (8, 7, 9, 6, 10, 5, 11, 4, 12, 3, 13, 2, 14, 1, 15)
+LOW_FIRST = (0, 1, 2, 3, 4, 5, 6, 7, 15, 14, 13, 12, 8, 11, 9, 10)
 PLANE = sorted(
     (
         (dy, dh, dl)
@@ -378,34 +379,35 @@
 
     recv(17, frecv.at[pl.ds(0, 15)])
     ysend[...] = jnp.sum(frecv[...].astype(F32), axis=0).astype(BF)
-
-    def y_copy(d, k):
-        to = {"z": wrap(z + d, NZ)}
-        return remote(ysend, yrecv.at[z], sent.at[k], came.at[k], to)
-
-    def y_pass(block, d):
-        part = yrecv.at[wrap(z + block, NZ)]
-        return remote(part, part, sent.at[21], came.at[21], {"z": wrap(z + d, NZ)})
-
-    for d in (5, 11):
-        y_copy(d, 11).start()
-    for d in (1, 15, 2, 14):
-        y_copy(d, 13).start()
-    yrecv[z] = ysend[...]
+    for t in range(5):
+
+        @pl.when(z != t)
+        def _():
+            remote(ysend.at[t], yrecv.at[z], sent.at[11], came.at[11], {"z": t}).start()
+
+        @pl.when(z == t)
+        def _():
+            yrecv[z] = ysend[t]
+
+    def low_first(copy):
+        for zz in LOW_FIRST:
+            pl.when(z != zz)(lambda: copy({"z": zz}).start())
+
+    def y_copy(to):
+        return remote(yall.at[z], yall.at[z], sent.at[13], came.at[13], to)
+
+    def zg_copy(to):
+        return remote(zall.at[z], zall.at[z], sent.at[12], came.at[12], to)
+
+    @pl.when(z < 5)
+    def _():
+        recv(11, yrecv.at[pl.ds(0, 15)])
+        yall[z] = jnp.sum(yrecv[...].astype(F32), axis=0).astype(BF)
+        low_first(y_copy)
 
     recv(10, zrecv.at[pl.ds(0, 15)])
     zall[z] = jnp.sum(zrecv[...].astype(F32), axis=0).astype(BF)
-
-    def zg_copy(peer):
-        return remote(zall.at[z], zall.at[z], sent.at[12], came.at[12], {"z": peer})
-
-    start_z(zg_copy)
-
-    recv(11, yrecv.at[pl.ds(0, 2)])
-    for d in (2, 14, 1, 15):
-        for block in (5, 11):
-            y_pass(block, d).start()
-    y_pass(11 - 6 * odd, 3 + 10 * odd).start()
+    low_first(zg_copy)
 
     recv(7, hrecv.at[pl.ds(0, 15)])
     dg_ref[...] = jnp.sum(hrecv[...].astype(F32), axis=0)
@@ -417,12 +419,19 @@
     )
     outs[0].start()
 
-    recv(13, yrecv.at[pl.ds(0, 4)])
-    recv(21, yrecv.at[pl.ds(0, 9)])
-    yall[...] = jnp.sum(yrecv[...].astype(F32), axis=0).astype(BF)
+    @pl.when(z < 5)
+    def _():
+        recv(13, yall.at[pl.ds(0, 4)])
+
+    @pl.when(z >= 5)
+    def _():
+        recv(13, yall.at[pl.ds(0, 5)])
+
     for d in PLANE:
-        remote(yall, fall.at[c, q], sent.at[15], came.at[15], plane(d)[1]).start()
-    fall[c, q] = yall[...]
+        remote(
+            yall.at[pl.ds(0, 5)], fall.at[c, q], sent.at[15], came.at[15], plane(d)[1]
+        ).start()
+    fall[c, q] = yall[0:5]
     tile[...] = yall[4]
     outs[1].start()
     recv(12, zall.at[pl.ds(0, 15)])
@@ -452,9 +461,15 @@
     left(18, qrecv)
     left(10, zrecv.at[pl.ds(0, 15)])
 
-    left(11, yrecv.at[pl.ds(0, 2)])
-    left(13, yrecv.at[pl.ds(0, 4)])
-    left(21, yrecv.at[pl.ds(0, 9)])
+    @pl.when(z < 5)
+    def _():
+        left(11, yall.at[pl.ds(0, 4)])
+        left(13, yrecv.at[pl.ds(0, 15)])
+
+    @pl.when(z >= 5)
+    def _():
+        left(11, yall.at[pl.ds(0, 5)])
+
     left(12, zrecv.at[pl.ds(0, 15)])
     left(14, zall)
     left(15, fall.at[0, pl.ds(0, 15)])
@@ -584,14 +599,14 @@
             pltpu.VMEM((NZ, 2, 8, R), BF),
             pltpu.VMEM((NZ, 2, 8, R), BF),
             pltpu.VMEM((5, 8, R), BF),
-            pltpu.VMEM((NZ, 5, 8, R), BF),
-            pltpu.VMEM((5, 8, R), BF),
+            pltpu.VMEM((NZ, 8, R), BF),
+            pltpu.VMEM((NZ, 8, R), BF),
             pltpu.VMEM((2, 2, NZ, 2, 8, R), BF),
             pltpu.VMEM((2, 16, 5, 8, R), BF),
             pltpu.VMEM((8, R), BF),
             pltpu.VMEM((8, H), F32),
-            dma((22,)),
-            dma((22,)),
+            dma((21,)),
+            dma((21,)),
             dma((8,)),
             dma((4,)),
         ],

time: 72.9 us -> 73.1 us (level)
  no operation moved by 1% of the time
where the time goes in v8:
time: 73.1 us; the launch traced here: 72.9 us
  Pallas kernels  72.2 us (99%)
    pallas_call x1, Pallas kernels, on_device(): pl.pallas_call(kernel, out_shape=raw, in_specs=[smem, vmem] + [hbm] * 8,...  70.2 us
    pallas_call x1, Pallas kernels, on_device(): pl.pallas_call(unfold, out_shape=final, in_specs=[hbm] * 4, out_specs=(hb...  2.04 us

profile of v8, /device:TPU:1, one launch (start us, length us, event | category | flops | bytes accessed | tf_op | source)
XLA Modules:
  0.0 72.9 jit_solution(13340661234980872737)
XLA Ops:
  0.6 70.2 %shard_map.128 = (bf16[2,2,16,2,8,128]{5,4,3,2,1,0:T(8,128)(2,1)}, bf16[2,16,5,8,128]{4,3,2,1,0:T(8,128)(2,1)}, bf16[8,128]{1,0:T(8,128)(2,1)}, f32[8,1024]{1,0:T(8,128)}) custom-call(s32[64]{0:T(128)} %ids_ref.1, s32[1,64]{1,0:T(1,128)} %bitcast.8, bf16[512,128]{1,0:T(8,128)(2,1)} %xs_hbm.1, bf16[512,8,128]{2,1,0:T(8,128)(2,1)} %jac_hbm.1, ...), custom_call_target="tpu_custom_call" | custom-call | tf_op jit(solution)/shard_map/pallas_call | solution.py:559
  70.8 2.0 %shard_map.129 = (f32[128,1024]{1,0:T(8,128)}, f32[8,128]{1,0:T(8,128)}, f32[1024,128]{1,0:T(8,128)}, f32[1,128]{1,0:T(1,128)}, f32[8,1024]{1,0:T(8,128)}) custom-call(bf16[2,2,16,2,8,128]{5,4,3,2,1,0:T(8,128)(2,1)} %get-tuple-element.14.hall_hbm, bf16[2,16,5,8,128]{4,3,2,1,0:T(8,128)(2,1)} %get-tuple-element.15.fall_hbm, ...), custom_call_target="tpu_custom_call" | custom-call | tf_op jit(solution)/shard_map/pallas_call | solution.py:635

commit v9 on v8

--- a/solution.py
+++ b/solution.py
@@ -335,9 +335,6 @@
     )
     pre_round = jnp.where(top, jnp.broadcast_to(pre_back, (16, R)), 0.0).astype(BF)
     both = jnp.concatenate([lin_round, pre_round], axis=0)
-    qsend[...] = dot(ft[...], both, TN).astype(BF).reshape(2, 4 * R, R)
-    remote(qsend.at[1 - c], qpart, sent.at[8], came.at[8], partner).start()
-
     low = dot(both, hw_ref[...], NT)
     tan_lower = low[0:R]
     pre_lower = low[R : R + 1] * first_slope - 2.0 * first_act * first_slope * jnp.sum(
@@ -357,16 +354,31 @@
             fsend[cc, k, 0:4] = fw[r0 : r0 + 32, l0 : l0 + R].reshape(4, 8, R).astype(BF)
             fsend[cc, k, 4] = tail[:, l0 : l0 + R].astype(BF)
     remote(fsend.at[1 - c], fpart, sent.at[9], came.at[9], partner).start()
-    recv(8, qpart)
-    halves = qsend[c].astype(F32) + qpart[...].astype(F32)
-    qsum[...] = halves.astype(BF).reshape(2, 2 * R, R)
-    remote(qsum.at[1 - xl], qrecv, sent.at[18], came.at[18], xside).start()
+    qsend[...] = dot(ft[...], both, TN).astype(BF).reshape(2, 4 * R, R)
+    remote(qsend.at[1 - c], qpart, sent.at[8], came.at[8], partner).start()
     recv(9, fpart)
     fsum[...] = (fsend[c].astype(F32) + fpart[...].astype(F32)).astype(BF)
     for d in PLANE:
         peer, to = plane(d)
         remote(fsum.at[peer], frecv.at[q], sent.at[17], came.at[17], to).start()
     frecv[q] = fsum[q]
+    recv(8, qpart)
+    halves = qsend[c].astype(F32) + qpart[...].astype(F32)
+    qsum[...] = halves.astype(BF).reshape(2, 2 * R, R)
+    remote(qsum.at[1 - xl], qrecv, sent.at[18], came.at[18], xside).start()
+
+    recv(17, frecv.at[pl.ds(0, 15)])
+    ysend[...] = jnp.sum(frecv[...].astype(F32), axis=0).astype(BF)
+    for t in range(5):
+
+        @pl.when(z != t)
+        def _():
+            remote(ysend.at[t], yrecv.at[z], sent.at[11], came.at[11], {"z": t}).start()
+
+        @pl.when(z == t)
+        def _():
+            yrecv[z] = ysend[t]
+
     recv(18, qrecv)
     quarter = qsum[xl].astype(F32) + qrecv[...].astype(F32)
     zsend[...] = quarter.reshape(NZ, 2, 8, R).astype(BF)
@@ -376,18 +388,6 @@
 
     start_z(zr_copy)
     zrecv[z] = zsend[z]
-
-    recv(17, frecv.at[pl.ds(0, 15)])
-    ysend[...] = jnp.sum(frecv[...].astype(F32), axis=0).astype(BF)
-    for t in range(5):
-
-        @pl.when(z != t)
-        def _():
-            remote(ysend.at[t], yrecv.at[z], sent.at[11], came.at[11], {"z": t}).start()
-
-        @pl.when(z == t)
-        def _():
-            yrecv[z] = ysend[t]
 
     def low_first(copy):
         for zz in LOW_FIRST:

time: 73.1 us -> 72.7 us (level)
  no operation moved by 1% of the time
where the time goes in v9:
time: 72.7 us; the launch traced here: 72.5 us
  Pallas kernels  71.8 us (99%)
    pallas_call x1, Pallas kernels, on_device(): pl.pallas_call(kernel, out_shape=raw, in_specs=[smem, vmem] + [hbm] * 8,...  69.8 us
    pallas_call x1, Pallas kernels, on_device(): pl.pallas_call(unfold, out_shape=final, in_specs=[hbm] * 4, out_specs=(hb...  2.04 us

profile of v9, /device:TPU:1, one launch (start us, length us, event | category | flops | bytes accessed | tf_op | source)
XLA Modules:
  0.0 72.5 jit_solution(164591904817906234)
XLA Ops:
  0.6 69.8 %shard_map.128 = (bf16[2,2,16,2,8,128]{5,4,3,2,1,0:T(8,128)(2,1)}, bf16[2,16,5,8,128]{4,3,2,1,0:T(8,128)(2,1)}, bf16[8,128]{1,0:T(8,128)(2,1)}, f32[8,1024]{1,0:T(8,128)}) custom-call(s32[64]{0:T(128)} %ids_ref.1, s32[1,64]{1,0:T(1,128)} %bitcast.8, bf16[512,128]{1,0:T(8,128)(2,1)} %xs_hbm.1, bf16[512,8,128]{2,1,0:T(8,128)(2,1)} %jac_hbm.1, ...), custom_call_target="tpu_custom_call" | custom-call | tf_op jit(solution)/shard_map/pallas_call | solution.py:559
  70.4 2.0 %shard_map.129 = (f32[128,1024]{1,0:T(8,128)}, f32[8,128]{1,0:T(8,128)}, f32[1024,128]{1,0:T(8,128)}, f32[1,128]{1,0:T(1,128)}, f32[8,1024]{1,0:T(8,128)}) custom-call(bf16[2,2,16,2,8,128]{5,4,3,2,1,0:T(8,128)(2,1)} %get-tuple-element.14.hall_hbm, bf16[2,16,5,8,128]{4,3,2,1,0:T(8,128)(2,1)} %get-tuple-element.15.fall_hbm, ...), custom_call_target="tpu_custom_call" | custom-call | tf_op jit(solution)/shard_map/pallas_call | solution.py:635

commit v10 on v9

--- a/solution.py
+++ b/solution.py
@@ -414,38 +414,10 @@
     outs = (
         pltpu.make_async_copy(dg_ref, dg_hbm, put.at[0]),
         pltpu.make_async_copy(tile, tile_hbm, put.at[1]),
-        pltpu.make_async_copy(hall, hall_hbm, put.at[2]),
-        pltpu.make_async_copy(fall, fall_hbm, put.at[3]),
+        pltpu.make_async_copy(hall, hall_hbm.at[c], put.at[2]),
+        pltpu.make_async_copy(fall, fall_hbm.at[c], put.at[3]),
     )
     outs[0].start()
-
-    @pl.when(z < 5)
-    def _():
-        recv(13, yall.at[pl.ds(0, 4)])
-
-    @pl.when(z >= 5)
-    def _():
-        recv(13, yall.at[pl.ds(0, 5)])
-
-    for d in PLANE:
-        remote(
-            yall.at[pl.ds(0, 5)], fall.at[c, q], sent.at[15], came.at[15], plane(d)[1]
-        ).start()
-    fall[c, q] = yall[0:5]
-    tile[...] = yall[4]
-    outs[1].start()
-    recv(12, zall.at[pl.ds(0, 15)])
-    remote(zall, hall.at[c, xl], sent.at[14], came.at[14], xside).start()
-    hall[c, xl] = zall[...]
-    recv(15, fall.at[0, pl.ds(0, 15)])
-    remote(fall.at[c], fall.at[c], sent.at[19], came.at[19], partner).start()
-    recv(14, zall)
-    remote(hall.at[c], hall.at[c], sent.at[20], came.at[20], partner).start()
-    recv(19, fall.at[0])
-    outs[3].start()
-    recv(20, hall.at[0])
-    outs[2].start()
-
     left(0, tbytes.at[pl.ds(0, 15)])
     left(1, dblk.at[0, pl.ds(0, 2)])
     left(16, dblk.at[0, pl.ds(0, 4)])
@@ -463,6 +435,33 @@
 
     @pl.when(z < 5)
     def _():
+        recv(13, yall.at[pl.ds(0, 4)])
+
+    @pl.when(z >= 5)
+    def _():
+        recv(13, yall.at[pl.ds(0, 5)])
+
+    for d in PLANE:
+        remote(
+            yall.at[pl.ds(0, 5)], fall.at[q], sent.at[15], came.at[15], plane(d)[1]
+        ).start()
+    fall[q] = yall[0:5]
+    tile[...] = yall[4]
+    outs[1].start()
+    recv(12, zall.at[pl.ds(0, 15)])
+    remote(zall, hall.at[xl], sent.at[14], came.at[14], xside).start()
+    hall[xl] = zall[...]
+    recv(15, fall.at[pl.ds(0, 15)])
+    remote(fall, fall_hbm.at[c], sent.at[19], came.at[19], partner).start()
+    outs[3].start()
+    recv(14, zall)
+    remote(hall, hall_hbm.at[c], sent.at[20], came.at[20], partner).start()
+    outs[2].start()
+    recv(19, fall)
+    recv(20, hall)
+
+    @pl.when(z < 5)
+    def _():
         left(11, yall.at[pl.ds(0, 4)])
         left(13, yrecv.at[pl.ds(0, 15)])
 
@@ -472,9 +471,9 @@
 
     left(12, zrecv.at[pl.ds(0, 15)])
     left(14, zall)
-    left(15, fall.at[0, pl.ds(0, 15)])
-    left(19, fall.at[0])
-    left(20, hall.at[0])
+    left(15, fall.at[pl.ds(0, 15)])
+    left(19, fall)
+    left(20, hall)
     for out in outs:
         out.wait()
 
@@ -601,8 +600,8 @@
             pltpu.VMEM((5, 8, R), BF),
             pltpu.VMEM((NZ, 8, R), BF),
             pltpu.VMEM((NZ, 8, R), BF),
-            pltpu.VMEM((2, 2, NZ, 2, 8, R), BF),
-            pltpu.VMEM((2, 16, 5, 8, R), BF),
+            pltpu.VMEM((2, NZ, 2, 8, R), BF),
+            pltpu.VMEM((16, 5, 8, R), BF),
             pltpu.VMEM((8, R), BF),
             pltpu.VMEM((8, H), F32),
             dma((21,)),

time: 72.7 us -> 72.1 us (level)
  no operation moved by 1% of the time
where the time goes in v10:
time: 72.1 us; the launch traced here: 71.9 us
  Pallas kernels  71.3 us (99%)
    pallas_call x1, Pallas kernels, on_device(): pl.pallas_call(kernel, out_shape=raw, in_specs=[smem, vmem] + [hbm] * 8,...  69.2 us
    pallas_call x1, Pallas kernels, on_device(): pl.pallas_call(unfold, out_shape=final, in_specs=[hbm] * 4, out_specs=(hb...  2.04 us

profile of v10, /device:TPU:1, one launch (start us, length us, event | category | flops | bytes accessed | tf_op | source)
XLA Modules:
  0.0 71.9 jit_solution(1344975677346515719)
XLA Ops:
  0.6 69.2 %shard_map.128 = (bf16[2,2,16,2,8,128]{5,4,3,2,1,0:T(8,128)(2,1)}, bf16[2,16,5,8,128]{4,3,2,1,0:T(8,128)(2,1)}, bf16[8,128]{1,0:T(8,128)(2,1)}, f32[8,1024]{1,0:T(8,128)}) custom-call(s32[64]{0:T(128)} %ids_ref.1, s32[1,64]{1,0:T(1,128)} %bitcast.8, bf16[512,128]{1,0:T(8,128)(2,1)} %xs_hbm.1, bf16[512,8,128]{2,1,0:T(8,128)(2,1)} %jac_hbm.1, ...), custom_call_target="tpu_custom_call" | custom-call | tf_op jit(solution)/shard_map/pallas_call | solution.py:558
  69.9 2.0 %shard_map.129 = (f32[128,1024]{1,0:T(8,128)}, f32[8,128]{1,0:T(8,128)}, f32[1024,128]{1,0:T(8,128)}, f32[1,128]{1,0:T(1,128)}, f32[8,1024]{1,0:T(8,128)}) custom-call(bf16[2,2,16,2,8,128]{5,4,3,2,1,0:T(8,128)(2,1)} %get-tuple-element.14.hall_hbm, bf16[2,16,5,8,128]{4,3,2,1,0:T(8,128)(2,1)} %get-tuple-element.15.fall_hbm, ...), custom_call_target="tpu_custom_call" | custom-call | tf_op jit(solution)/shard_map/pallas_call | solution.py:634

commit v11 on v10

--- a/solution.py
+++ b/solution.py
@@ -512,11 +512,8 @@
         pltpu.make_async_copy(hb, hb_hbm, put.at[3]),
         pltpu.make_async_copy(fb, fb_hbm, put.at[4]),
     )
-    for copy in ins:
-        copy.start()
-    ins[0].wait()
-    hg[...] = hall[...].astype(F32).reshape(H, R)
-    outs[0].start()
+    for k in (1, 0, 3, 2):
+        ins[k].start()
     ins[1].wait()
     for mm in range(8):
         for ee in range(4):
@@ -526,11 +523,14 @@
                 fb[mm : mm + 1, :] = piece[4, 0:1]
     outs[1].start()
     outs[4].start()
-    ins[2].wait()
-    outs[2].start()
     ins[3].wait()
     hb[...] = tile[...].astype(F32)[1:2]
     outs[3].start()
+    ins[2].wait()
+    outs[2].start()
+    ins[0].wait()
+    hg[...] = hall[...].astype(F32).reshape(H, R)
+    outs[0].start()
     for copy in outs:
         copy.wait()
 

time: 72.1 us -> 72.2 us (level)
  no operation moved by 1% of the time
where the time goes in v11:
time: 72.2 us; the launch traced here: 72 us
  Pallas kernels  71.3 us (99%)
    pallas_call x1, Pallas kernels, on_device(): pl.pallas_call(kernel, out_shape=raw, in_specs=[smem, vmem] + [hbm] * 8,...  69.2 us
    pallas_call x1, Pallas kernels, on_device(): pl.pallas_call(unfold, out_shape=final, in_specs=[hbm] * 4, out_specs=(hb...  2.1 us

profile of v11, /device:TPU:1, one launch (start us, length us, event | category | flops | bytes accessed | tf_op | source)
XLA Modules:
  0.0 72.0 jit_solution(5338885763511338309)
XLA Ops:
  0.6 69.2 %shard_map.128 = (bf16[2,2,16,2,8,128]{5,4,3,2,1,0:T(8,128)(2,1)}, bf16[2,16,5,8,128]{4,3,2,1,0:T(8,128)(2,1)}, bf16[8,128]{1,0:T(8,128)(2,1)}, f32[8,1024]{1,0:T(8,128)}) custom-call(s32[64]{0:T(128)} %ids_ref.1, s32[1,64]{1,0:T(1,128)} %bitcast.8, bf16[512,128]{1,0:T(8,128)(2,1)} %xs_hbm.1, bf16[512,8,128]{2,1,0:T(8,128)(2,1)} %jac_hbm.1, ...), custom_call_target="tpu_custom_call" | custom-call | tf_op jit(solution)/shard_map/pallas_call | solution.py:558
  69.9 2.1 %shard_map.129 = (f32[128,1024]{1,0:T(8,128)}, f32[8,128]{1,0:T(8,128)}, f32[1024,128]{1,0:T(8,128)}, f32[1,128]{1,0:T(1,128)}, f32[8,1024]{1,0:T(8,128)}) custom-call(bf16[2,2,16,2,8,128]{5,4,3,2,1,0:T(8,128)(2,1)} %get-tuple-element.14.hall_hbm, bf16[2,16,5,8,128]{4,3,2,1,0:T(8,128)(2,1)} %get-tuple-element.15.fall_hbm, ...), custom_call_target="tpu_custom_call" | custom-call | tf_op jit(solution)/shard_map/pallas_call | solution.py:634
